TPU v7x, 32 devices: a whole 2x2x4 slice. The times are simulated.
32 devices in a mesh: row: 8 (over y, x, core), col: 4 (over z).
Axes of the slice: x: 2, y: 2, z: 4, core: 2. Of those that a mesh axis runs over, the one named last changes fastest.
Arguments:
- pair: bfloat16 [256, 256, 128], P('row', 'col'), may hold values from -6 to 6
- group: bfloat16 [32, 256, 128], P('col', 'row'), may hold values from -6 to 6
- w_query: bfloat16 [128, 128], replicated, may hold values from -0.5 to 0.5
- w_key: bfloat16 [128, 128], replicated, may hold values from -0.5 to 0.5
- w_value: bfloat16 [128, 128], replicated, may hold values from -0.5 to 0.5
- w_gate: bfloat16 [128, 128], replicated, may hold values from -0.5 to 0.5
- w_bias: float32 [128, 4], replicated, may hold values from -40 to 40
- w_out: bfloat16 [128, 128], replicated, may hold values from -0.5 to 0.5
Outputs:
- update: bfloat16 [32, 256, 128], P('col', 'row')
All inputs are finite; a program needn't handle non-finite values.
Results may differ from a plain program's by a relative error of at most 0.012.
Values may be sent and summed in bfloat16 or wider, within the bound.
No kernel may reach another device: no remote copies, remote signals or barrier semaphores. Data moves between devices by JAX's collectives and lax.ppermute only.
A program may use at most 64 MiB of HBM per device.

v0:
```python
import math

import jax
import jax.numpy as jnp
from jax import lax
from jax.experimental import pallas as pl
from jax.experimental.pallas import tpu as pltpu
from jax.sharding import PartitionSpec as P


EPS = 1e-05
NT = (((1,), (1,)), ((), ()))
GRANT = 16 << 20
VMEM = pl.BlockSpec(memory_space=pltpu.VMEM)


def call(kernel, outs, args, flops, scratch=(), space=pltpu.VMEM):
    return pl.pallas_call(
        kernel,
        out_shape=outs,
        in_specs=[pl.BlockSpec(memory_space=space)] * len(args),
        out_specs=jax.tree.map(lambda _: VMEM, outs),
        scratch_shapes=list(scratch),
        cost_estimate=pl.CostEstimate(flops=flops, bytes_accessed=1 << 20, transcendentals=0),
        compiler_params=pltpu.CompilerParams(vmem_limit_bytes=GRANT),
    )(*args)


def dot(a, b):
    return jnp.dot(a, b, preferred_element_type=jnp.float32)


def split(value):
    high = value.astype(jnp.bfloat16)
    return high, value - high.astype(jnp.float32)


def front_kernel(*refs):
    sources, (normed_ref, out_ref), landed, semaphores = refs[:3], refs[3:5], refs[5:8], refs[8]
    copies = [
        pltpu.make_async_copy(a, b, semaphores.at[i])
        for i, (a, b) in enumerate(zip(sources, landed))
    ]
    for copy in copies:
        copy.start()
    group_ref, pair_ref, w_ref = landed
    copies[0].wait()
    rows = group_ref[...].astype(jnp.float32)
    centered = rows - jnp.mean(rows, axis=-1, keepdims=True)
    spread = jnp.mean(centered * centered, axis=-1, keepdims=True)
    normed_ref[...] = (centered * lax.rsqrt(spread + EPS)).astype(jnp.bfloat16)
    copies[1].wait()
    copies[2].wait()
    cols, keys, channels = pair_ref.shape
    heads = w_ref.shape[0]
    half = cols // 2
    w = jnp.concatenate([w_ref[...]] * (8 // heads), axis=0)
    w_high, rest = split(w)
    w_mid, rest = split(rest)
    w_sum = jnp.sum(w, axis=1, keepdims=True)
    even = jnp.full((channels, channels), 1.0 / channels, jnp.bfloat16)
    blank = jnp.zeros((channels, channels), jnp.bfloat16)
    averages = jnp.concatenate(
        [jnp.concatenate([even, blank], axis=1), jnp.concatenate([blank, even], axis=1)], axis=0
    )
    pieces = jnp.concatenate([w_high, w_mid, rest.astype(jnp.bfloat16), even[:8]], axis=0)
    left = jnp.concatenate(
        [
            jnp.concatenate([pieces, blank[:96]], axis=0),
            jnp.concatenate([blank[:64], pieces, blank[:32]], axis=0),
        ],
        axis=1,
    )
    tiles = [
        jnp.concatenate([pair_ref[low], pair_ref[low + half]], axis=0) for low in range(half)
    ]
    twins = jnp.concatenate(
        [jnp.concatenate(tiles[low : low + 2], axis=1) for low in range(0, half, 2)], axis=0
    )
    means = dot(twins, averages)
    products = lax.dot_general(twins, left, NT, preferred_element_type=jnp.float32)
    height = 2 * keys
    lane = lax.broadcasted_iota(jnp.int32, (height, 128), 1)
    for low in range(0, half, 2):
        rows = slice(low // 2 * height, low // 2 * height + height)
        centered = twins[rows].astype(jnp.float32) - means[rows]
        squares = centered * centered
        first = jnp.sum(squares[:, :channels], axis=1, keepdims=True)
        second = jnp.sum(squares[:, channels:], axis=1, keepdims=True)
        mixed = jnp.where(
            (lane & 32) == 0, products[rows], jnp.where(lane < 64, first, second)
        ).T
        for twin in range(2):
            t = mixed[twin * 64 : twin * 64 + 64]
            total = t[0:8] + t[8:16] + t[16:24] - t[24:32] * w_sum
            bias = total * lax.rsqrt(t[32:40] * (1.0 / channels) + EPS)
            at = low + twin
            out_ref[pl.ds((at // 8) * 8 * heads + at % 8, heads, stride=8), :] = bias[0:heads]


def scores_kernel(heads, parts, *refs):
    blocks = refs[:parts]
    wq_ref, wk_ref, wv_ref, wg_ref, score_ref, value_ref, gate_ref, key_ref = refs[parts:]
    rows, cols, channels = blocks[0].shape
    width = wq_ref.shape[1]
    depth = width // heads
    me = lax.axis_index("row")
    own = blocks[0][...].reshape(rows * cols, channels)
    both = dot(own, jnp.concatenate([wq_ref[...], wg_ref[...]], axis=1))
    gate_ref[...] = jax.nn.sigmoid(both[:, width:]).reshape(rows, cols, width)
    query = both[:, :width] * (1.0 / math.sqrt(depth))
    w_kv = jnp.concatenate([wk_ref[...], wv_ref[...]], axis=1)
    for step in range(parts):
        block = blocks[step][...].reshape(rows * cols, channels)
        place = pl.ds(pl.multiple_of((me ^ step) * cols, cols), cols)
        kv = dot(block, w_kv).astype(jnp.bfloat16).reshape(rows, cols, 2 * width)
        key_ref[:, place, :] = kv[:, :, :width]
        value_ref[:, place, :] = kv[:, :, width:]
    lane = lax.broadcasted_iota(jnp.int32, (8, width), 1) // depth
    for row in range(rows):
        tiles = []
        for g in range(cols // 8):
            tile = query[row * cols + g * 8 : row * cols + g * 8 + 8]
            for h in range(heads):
                tiles.append(jnp.where(lane == h, tile, 0.0))
        stacked = jnp.concatenate(tiles, axis=0).astype(jnp.bfloat16)
        score_ref[row] = lax.dot_general(
            stacked, key_ref[row], NT, preferred_element_type=jnp.float32
        )


def attention_kernel(heads, parts, *refs):
    panels = refs[:parts]
    score_ref, value_ref, gate_ref, wo_ref, out_ref, bias_ref, hidden_ref = refs[parts:]
    rows, cols, width = gate_ref.shape
    depth = width // heads
    keys = panels[0].shape[1] // 2
    half = panels[0].shape[0]
    me = lax.axis_index("col")
    p = [r[...] for r in panels]
    bit = 1
    while bit < parts:
        flip = (me & bit) != 0
        p = [jnp.where(flip, p[s ^ bit], p[s]) for s in range(parts)]
        bit *= 2
    for h in range(2):
        for c in range(0, parts, 2):
            bias_ref[h * half : (h + 1) * half, c * keys : (c + 2) * keys] = jnp.concatenate(
                [x[:, h * keys : (h + 1) * keys] for x in p[c : c + 2]], axis=1
            )
    lane = lax.broadcasted_iota(jnp.int32, (8, width), 1) // depth
    ones = jnp.ones((value_ref.shape[1], width), jnp.bfloat16)
    for row in range(rows):
        scores = score_ref[row] + bias_ref[...]
        top = jnp.max(scores, axis=1, keepdims=True)
        weights = jnp.exp(scores - top).astype(jnp.bfloat16)
        both = dot(weights, jnp.concatenate([value_ref[row], ones], axis=1))
        for g in range(cols // 8):
            base = g * heads * 8
            pick = both[base : base + 8]
            for h in range(1, heads):
                tile = both[base + h * 8 : base + h * 8 + 8]
                keep = lane == h
                pick = jnp.where(jnp.concatenate([keep, keep], axis=1), tile, pick)
            mixed = pick[:, :width] / pick[:, width:]
            hidden_ref[row * cols + g * 8 : row * cols + g * 8 + 8] = (
                gate_ref[row, g * 8 : g * 8 + 8] * mixed
            )
    result = dot(hidden_ref[...].astype(jnp.bfloat16), wo_ref[...])
    out_ref[...] = result.astype(jnp.bfloat16).reshape(out_ref.shape)


def swap(value, axis, size, distance):
    return lax.ppermute(value, axis, [(i, i ^ distance) for i in range(size)])


def per_device(row_size, col_size, pair, group, w_query, w_key, w_value, w_gate, w_bias, w_out):
    heads = w_bias.shape[1]
    rows, cols, _ = group.shape
    width = w_query.shape[1]
    keys = pair.shape[1]
    all_keys = row_size * cols
    shape = jax.ShapeDtypeStruct
    normed, panel = call(
        front_kernel,
        (
            shape(group.shape, jnp.bfloat16),
            shape((cols * heads // 2, 2 * keys), jnp.float32),
        ),
        [pltpu.with_memory_space_constraint(a, pltpu.HBM) for a in (group, pair, w_bias.T)],
        2 * 10**9,
        [pltpu.VMEM(a.shape, a.dtype) for a in (group, pair, w_bias.T)]
        + [pltpu.SemaphoreType.DMA((3,))],
        pltpu.HBM,
    )
    blocks = {0: normed}
    for s in range(2, row_size, 2):
        blocks[s] = swap(normed, "row", row_size, s)
    for s in range(0, row_size, 2):
        blocks[s + 1] = swap(blocks[s], "row", row_size, 1)
    panels = [panel] + [swap(panel, "col", col_size, s) for s in range(1, col_size)]
    scores, value, gate = call(
        lambda *refs: scores_kernel(heads, row_size, *refs),
        (
            shape((rows, cols * heads, all_keys), jnp.float32),
            shape((rows, all_keys, width), jnp.bfloat16),
            shape((rows, cols, width), jnp.float32),
        ),
        [blocks[s] for s in range(row_size)] + [w_query, w_key, w_value, w_gate],
        10**9,
        [pltpu.VMEM((rows, all_keys, width), jnp.bfloat16)],
    )
    return call(
        lambda *refs: attention_kernel(heads, col_size, *refs),
        shape((rows, cols, w_out.shape[1]), jnp.bfloat16),
        panels + [scores, value, gate, w_out],
        10**9,
        [
            pltpu.VMEM((cols * heads, all_keys), jnp.float32),
            pltpu.VMEM((rows * cols, width), jnp.float32),
        ],
    )


def solution(mesh):
    row_size, col_size = mesh.shape["row"], mesh.shape["col"]
    in_specs = (P("row", "col", None), P("col", "row", None), P(), P(), P(), P(), P(), P())

    def body(*args):
        return per_device(row_size, col_size, *args)

    return jax.shard_map(
        body,
        mesh=mesh,
        in_specs=in_specs,
        out_specs=P("col", "row", None),
        check_vma=False,
    )
```

profile of v0, /device:TPU:0, one launch (start us, length us, event | category | flops | bytes accessed | tf_op | source)
XLA Modules:
  0.0 22.8 jit_solution(13856043251456409861)
XLA Ops:
  0.0 0.0 copy-start
  0.0 0.0 copy-start.1
  0.0 0.0 copy-start.2
  0.0 0.0 copy-start.3
  0.0 1.9 %shard_map.82 = (bf16[8,32,128]{2,1,0:T(8,128)(2,1)S(1)}, f32[64,128]{1,0:T(8,128)S(1)}) custom-call(bf16[8,32,128]{2,1,0:T(8,128)(2,1)} %refs_0_.1, bf16[32,64,128]{2,1,0:T(8,128)(2,1)} %refs_1_.1, f32[4,128]{1,0:T(4,128)} %bitcast.1), custom_call_target="tpu_custom_call" | custom-call | flops 2000000000 | bytes 1048576 | tf_op jit(solution)/shard_map/pallas_call | solution.py:18
  1.9 3.1 %collective-permute-start.4 = (bf16[8,32,128]{2,1,0:T(8,128)(2,1)S(1)}, bf16[8,32,128]{2,1,0:T(8,128)(2,1)S(1)}, u32[]{:S(2)}, u32[]{:S(2)}) collective-permute-start(bf16[8,32,128]{2,1,0:T(8,128)(2,1)S(1)} %get-tuple-element.11.refs_0_), channel_id=1, source_target_pairs={{0,8},{4,12},{8,0},{12,4},{16,24},{20,28},{24,16},{28,20},{1,9},{5... | collective-permute-start | bytes 196616 | tf_op jit(solution)/shard_map/ppermute | solution.py:174
  5.0 1.5 %collective-permute-start.6 = (bf16[8,32,128]{2,1,0:T(8,128)(2,1)S(1)}, bf16[8,32,128]{2,1,0:T(8,128)(2,1)S(1)}, u32[]{:S(2)}, u32[]{:S(2)}) collective-permute-start(bf16[8,32,128]{2,1,0:T(8,128)(2,1)S(1)} %get-tuple-element.11.refs_0_), channel_id=1, source_target_pairs={{0,16},{4,20},{8,24},{12,28},{16,0},{20,4},{24,8},{28,12},{1,17},{... | collective-permute-start | bytes 196616 | tf_op jit(solution)/shard_map/ppermute | solution.py:174
  6.5 0.0 collective-permute-start.8
  6.5 0.0 collective-permute-start.3
  6.6 0.8 %collective-permute-done.4.refs_2_ = bf16[8,32,128]{2,1,0:T(8,128)(2,1)S(1)} collective-permute-done((bf16[8,32,128]{2,1,0:T(8,128)(2,1)S(1)}, bf16[8,32,128]{2,1,0:T(8,128)(2,1)S(1)}, u32[]{:S(2)}, u32[]{:S(2)}) %collective-permute-start.4) | collective-permute-done | bytes 65568 | tf_op jit(solution)/shard_map/ppermute | solution.py:174
  7.4 0.0 collective-permute-start.5
  7.4 1.9 %collective-permute-done.6.refs_4_ = bf16[8,32,128]{2,1,0:T(8,128)(2,1)S(1)} collective-permute-done((bf16[8,32,128]{2,1,0:T(8,128)(2,1)S(1)}, bf16[8,32,128]{2,1,0:T(8,128)(2,1)S(1)}, u32[]{:S(2)}, u32[]{:S(2)}) %collective-permute-start.6) | collective-permute-done | bytes 65568 | tf_op jit(solution)/shard_map/ppermute | solution.py:174
  9.3 0.0 collective-permute-start.7
  9.3 2.4 %collective-permute-done.8.refs_6_ = bf16[8,32,128]{2,1,0:T(8,128)(2,1)S(1)} collective-permute-done((bf16[8,32,128]{2,1,0:T(8,128)(2,1)S(1)}, bf16[8,32,128]{2,1,0:T(8,128)(2,1)S(1)}, u32[]{:S(2)}, u32[]{:S(2)}) %collective-permute-start.8) | collective-permute-done | bytes 65568 | tf_op jit(solution)/shard_map/ppermute | solution.py:174
  11.7 0.0 collective-permute-start.9
  11.7 0.0 copy-start.4
  11.7 1.6 %collective-permute-start = (f32[64,128]{1,0:T(8,128)S(1)}, f32[64,128]{1,0:T(8,128)S(1)}, u32[]{:S(2)}, u32[]{:S(2)}) collective-permute-start(f32[64,128]{1,0:T(8,128)S(1)} %get-tuple-element.10.refs_0_), channel_id=1, source_target_pairs={{0,1},{1,0},{2,3},{3,2},{4,5},{5,4},{6,7},{7,6},{8,9},{9,8},{10,11... | collective-permute-start | bytes 98312 | tf_op jit(solution)/shard_map/ppermute | solution.py:174
  13.3 0.0 collective-permute-done.3.refs_1_
  13.3 2.6 %collective-permute-start.1 = (f32[64,128]{1,0:T(8,128)S(1)}, f32[64,128]{1,0:T(8,128)S(1)}, u32[]{:S(2)}, u32[]{:S(2)}) collective-permute-start(f32[64,128]{1,0:T(8,128)S(1)} %get-tuple-element.10.refs_0_), channel_id=1, source_target_pairs={{0,2},{1,3},{2,0},{3,1},{4,6},{5,7},{6,4},{7,5},{8,10},{9,11},{10,... | collective-permute-start | bytes 98312 | tf_op jit(solution)/shard_map/ppermute | solution.py:174
  15.9 0.0 collective-permute-done.5.refs_3_
  15.9 0.2 collective-permute-start.2
  16.1 0.0 collective-permute-done.7.refs_5_
  16.1 0.0 collective-permute-done.9.refs_7_
  16.1 0.0 copy-done
  16.1 0.0 copy-done.1
  16.1 0.0 copy-done.2
  16.1 0.0 copy-done.3
  16.1 0.8 %shard_map.83 = (f32[8,128,256]{2,1,0:T(8,128)S(1)}, bf16[8,256,128]{2,1,0:T(8,128)(2,1)S(1)}, f32[8,32,128]{2,1,0:T(8,128)S(1)}) custom-call(bf16[8,32,128]{2,1,0:T(8,128)(2,1)S(1)} %get-tuple-element.11.refs_0_, bf16[8,32,128]{2,1,0:T(8,128)(2,1)S(1)} %collective-permute-done.3.refs_1_, bf16[8,32,128]{2,1,0:T(8,128)(2,1)S(1)} %collective-permute-done.4.refs_2_, ...), custom_call_target="tpu_custom_call" | custom-call | flops 1000000000 | bytes 1048576 | tf_op jit(solution)/shard_map/pallas_call | solution.py:18
  17.0 0.0 collective-permute-done.refs_1_
  17.0 1.6 %collective-permute-done.1.refs_2_ = f32[64,128]{1,0:T(8,128)S(1)} collective-permute-done((f32[64,128]{1,0:T(8,128)S(1)}, f32[64,128]{1,0:T(8,128)S(1)}, u32[]{:S(2)}, u32[]{:S(2)}) %collective-permute-start.1) | collective-permute-done | bytes 32800 | tf_op jit(solution)/shard_map/ppermute | solution.py:174
  18.6 3.0 %collective-permute-done.2.refs_3_ = f32[64,128]{1,0:T(8,128)S(1)} collective-permute-done((f32[64,128]{1,0:T(8,128)S(1)}, f32[64,128]{1,0:T(8,128)S(1)}, u32[]{:S(2)}, u32[]{:S(2)}) %collective-permute-start.2) | collective-permute-done | bytes 32800 | tf_op jit(solution)/shard_map/ppermute | solution.py:174
  21.6 0.0 copy-done.4
  21.6 1.2 %shard_map.84 = bf16[8,32,128]{2,1,0:T(8,128)(2,1)} custom-call(f32[64,128]{1,0:T(8,128)S(1)} %get-tuple-element.10.refs_0_, f32[64,128]{1,0:T(8,128)S(1)} %collective-permute-done.refs_1_, f32[64,128]{1,0:T(8,128)S(1)} %collective-permute-done.1.refs_2_, f32[64,128]{1,0:T(8,128)S(1)} %collective-permute-done.2.refs_3_, ...), custom_call_target="tpu_custom_call" | custom-call | flops 1000000000 | bytes 1048576 | tf_op jit(solution)/shard_map/pallas_call | solution.py:18
Async XLA Ops:
  0.0 16.1 %copy-start = (bf16[128,128]{1,0:T(8,128)(2,1)S(1)}, bf16[128,128]{1,0:T(8,128)(2,1)}, u32[]{:S(2)}) copy-start(bf16[128,128]{1,0:T(8,128)(2,1)} %refs_8_.1) | copy-start | bytes 98308
  0.0 16.1 %copy-start.1 = (bf16[128,128]{1,0:T(8,128)(2,1)S(1)}, bf16[128,128]{1,0:T(8,128)(2,1)}, u32[]{:S(2)}) copy-start(bf16[128,128]{1,0:T(8,128)(2,1)} %refs_9_.1) | copy-start | bytes 98308
  0.0 16.1 %copy-start.2 = (bf16[128,128]{1,0:T(8,128)(2,1)S(1)}, bf16[128,128]{1,0:T(8,128)(2,1)}, u32[]{:S(2)}) copy-start(bf16[128,128]{1,0:T(8,128)(2,1)} %refs_10_.1) | copy-start | bytes 98308
  0.0 16.1 %copy-start.3 = (bf16[128,128]{1,0:T(8,128)(2,1)S(1)}, bf16[128,128]{1,0:T(8,128)(2,1)}, u32[]{:S(2)}) copy-start(bf16[128,128]{1,0:T(8,128)(2,1)} %refs_11_.1) | copy-start | bytes 98308
  1.9 5.4 %collective-permute-start.4 = (bf16[8,32,128]{2,1,0:T(8,128)(2,1)S(1)}, bf16[8,32,128]{2,1,0:T(8,128)(2,1)S(1)}, u32[]{:S(2)}, u32[]{:S(2)}) collective-permute-start(bf16[8,32,128]{2,1,0:T(8,128)(2,1)S(1)} %get-tuple-element.11.refs_0_), channel_id=1, source_target_pairs={{0,8},{4,12},{8,0},{12,4},{16,24},{20,28},{24,16},{28,20},{1,9},{5... | collective-permute-start | bytes 196616 | tf_op jit(solution)/shard_map/ppermute | solution.py:174
  5.0 4.3 %collective-permute-start.6 = (bf16[8,32,128]{2,1,0:T(8,128)(2,1)S(1)}, bf16[8,32,128]{2,1,0:T(8,128)(2,1)S(1)}, u32[]{:S(2)}, u32[]{:S(2)}) collective-permute-start(bf16[8,32,128]{2,1,0:T(8,128)(2,1)S(1)} %get-tuple-element.11.refs_0_), channel_id=1, source_target_pairs={{0,16},{4,20},{8,24},{12,28},{16,0},{20,4},{24,8},{28,12},{1,17},{... | collective-permute-start | bytes 196616 | tf_op jit(solution)/shard_map/ppermute | solution.py:174
  6.5 5.2 %collective-permute-start.8 = (bf16[8,32,128]{2,1,0:T(8,128)(2,1)S(1)}, bf16[8,32,128]{2,1,0:T(8,128)(2,1)S(1)}, u32[]{:S(2)}, u32[]{:S(2)}) collective-permute-start(bf16[8,32,128]{2,1,0:T(8,128)(2,1)S(1)} %get-tuple-element.11.refs_0_), channel_id=1, source_target_pairs={{0,24},{4,28},{8,16},{12,20},{16,8},{20,12},{24,0},{28,4},{1,25},{... | collective-permute-start | bytes 196616 | tf_op jit(solution)/shard_map/ppermute | solution.py:174
  6.5 6.7 %collective-permute-start.3 = (bf16[8,32,128]{2,1,0:T(8,128)(2,1)S(1)}, bf16[8,32,128]{2,1,0:T(8,128)(2,1)S(1)}, u32[]{:S(2)}, u32[]{:S(2)}) collective-permute-start(bf16[8,32,128]{2,1,0:T(8,128)(2,1)S(1)} %get-tuple-element.11.refs_0_), channel_id=1, source_target_pairs={{0,4},{4,0},{8,12},{12,8},{16,20},{20,16},{24,28},{28,24},{1,5},{5... | collective-permute-start | bytes 196616 | tf_op jit(solution)/shard_map/ppermute | solution.py:174
  7.4 8.5 %collective-permute-start.5 = (bf16[8,32,128]{2,1,0:T(8,128)(2,1)S(1)}, bf16[8,32,128]{2,1,0:T(8,128)(2,1)S(1)}, u32[]{:S(2)}, u32[]{:S(2)}) collective-permute-start(bf16[8,32,128]{2,1,0:T(8,128)(2,1)S(1)} %collective-permute-done.4.refs_2_), channel_id=1, source_target_pairs={{0,4},{4,0},{8,12},{12,8},{16,20},{20,16},{24,28},{28,24},{1,5},{5... | collective-permute-start | bytes 196616 | tf_op jit(solution)/shard_map/ppermute | solution.py:174
  9.3 6.8 %collective-permute-start.7 = (bf16[8,32,128]{2,1,0:T(8,128)(2,1)S(1)}, bf16[8,32,128]{2,1,0:T(8,128)(2,1)S(1)}, u32[]{:S(2)}, u32[]{:S(2)}) collective-permute-start(bf16[8,32,128]{2,1,0:T(8,128)(2,1)S(1)} %collective-permute-done.6.refs_4_), channel_id=1, source_target_pairs={{0,4},{4,0},{8,12},{12,8},{16,20},{20,16},{24,28},{28,24},{1,5},{5... | collective-permute-start | bytes 196616 | tf_op jit(solution)/shard_map/ppermute | solution.py:174
  11.7 4.4 %collective-permute-start.9 = (bf16[8,32,128]{2,1,0:T(8,128)(2,1)S(1)}, bf16[8,32,128]{2,1,0:T(8,128)(2,1)S(1)}, u32[]{:S(2)}, u32[]{:S(2)}) collective-permute-start(bf16[8,32,128]{2,1,0:T(8,128)(2,1)S(1)} %collective-permute-done.8.refs_6_), channel_id=1, source_target_pairs={{0,4},{4,0},{8,12},{12,8},{16,20},{20,16},{24,28},{28,24},{1,5},{5... | collective-permute-start | bytes 196616 | tf_op jit(solution)/shard_map/ppermute | solution.py:174
  11.7 9.9 %copy-start.4 = (bf16[128,128]{1,0:T(8,128)(2,1)S(1)}, bf16[128,128]{1,0:T(8,128)(2,1)}, u32[]{:S(2)}) copy-start(bf16[128,128]{1,0:T(8,128)(2,1)} %refs_7_.1) | copy-start | bytes 98308
  11.7 5.3 %collective-permute-start = (f32[64,128]{1,0:T(8,128)S(1)}, f32[64,128]{1,0:T(8,128)S(1)}, u32[]{:S(2)}, u32[]{:S(2)}) collective-permute-start(f32[64,128]{1,0:T(8,128)S(1)} %get-tuple-element.10.refs_0_), channel_id=1, source_target_pairs={{0,1},{1,0},{2,3},{3,2},{4,5},{5,4},{6,7},{7,6},{8,9},{9,8},{10,11... | collective-permute-start | bytes 98312 | tf_op jit(solution)/shard_map/ppermute | solution.py:174
  13.3 5.3 %collective-permute-start.1 = (f32[64,128]{1,0:T(8,128)S(1)}, f32[64,128]{1,0:T(8,128)S(1)}, u32[]{:S(2)}, u32[]{:S(2)}) collective-permute-start(f32[64,128]{1,0:T(8,128)S(1)} %get-tuple-element.10.refs_0_), channel_id=1, source_target_pairs={{0,2},{1,3},{2,0},{3,1},{4,6},{5,7},{6,4},{7,5},{8,10},{9,11},{10,... | collective-permute-start | bytes 98312 | tf_op jit(solution)/shard_map/ppermute | solution.py:174
  15.9 5.7 %collective-permute-start.2 = (f32[64,128]{1,0:T(8,128)S(1)}, f32[64,128]{1,0:T(8,128)S(1)}, u32[]{:S(2)}, u32[]{:S(2)}) collective-permute-start(f32[64,128]{1,0:T(8,128)S(1)} %get-tuple-element.10.refs_0_), channel_id=1, source_target_pairs={{0,3},{1,2},{2,1},{3,0},{4,7},{5,6},{6,5},{7,4},{8,11},{9,10},{10,... | collective-permute-start | bytes 98312 | tf_op jit(solution)/shard_map/ppermute | solution.py:174
where the time goes:
time: 22.9 us; the launch traced here: 22.8 us
  waiting for transfers between devices  9.75 us (43%)
  starting transfers between devices  9 us (39%)
  Pallas kernels  3.95 us (17%)
    ppermute x10, waiting for transfers between devices, swap(): return lax.ppermute(value, axis, [(i, i ^ distance) for i in range(size)])  9.75 us
    ppermute x10, starting transfers between devices, swap(): return lax.ppermute(value, axis, [(i, i ^ distance) for i in range(size)])  9 us
    pallas_call x3, Pallas kernels, call(): pl.pallas_call(kernel, out_shape=outs, in_specs=[pl.BlockSpec(memory_spac...  3.95 us
  transfers between devices with their start and end apart: 10, of which 5 were waited for; matrix products, arithmetic and copies ran while one was open for 0% of the time, Pallas kernels for 4%

commit v1 on v0

--- a/solution.py
+++ b/solution.py
@@ -98,21 +98,28 @@
             out_ref[pl.ds((at // 8) * 8 * heads + at % 8, heads, stride=8), :] = bias[0:heads]
 
 
-def scores_kernel(heads, parts, *refs):
-    blocks = refs[:parts]
-    wq_ref, wk_ref, wv_ref, wg_ref, score_ref, value_ref, gate_ref, key_ref = refs[parts:]
-    rows, cols, channels = blocks[0].shape
+def scores_kernel(heads, origins, *refs):
+    sources = len(origins)
+    wq_ref, wk_ref, wv_ref, wg_ref, score_ref, value_ref, gate_ref, key_ref = refs[sources:]
+    _, rows, cols, channels = refs[0].shape
     width = wq_ref.shape[1]
     depth = width // heads
     me = lax.axis_index("row")
-    own = blocks[0][...].reshape(rows * cols, channels)
+    chips = key_ref.shape[1] // (2 * cols)
+    own = refs[0][0].reshape(rows * cols, channels)
     both = dot(own, jnp.concatenate([wq_ref[...], wg_ref[...]], axis=1))
     gate_ref[...] = jax.nn.sigmoid(both[:, width:]).reshape(rows, cols, width)
     query = both[:, :width] * (1.0 / math.sqrt(depth))
     w_kv = jnp.concatenate([wk_ref[...], wv_ref[...]], axis=1)
-    for step in range(parts):
-        block = blocks[step][...].reshape(rows * cols, channels)
-        place = pl.ds(pl.multiple_of((me ^ step) * cols, cols), cols)
+    for ref, entry, (flip, odd, even) in [
+        (ref, entry, origin)
+        for ref, group in zip(refs, origins)
+        for entry, origin in enumerate(group)
+    ]:
+        block = ref[entry].reshape(rows * cols, channels)
+        core = me & 1
+        chip = lax.rem((me >> 1) + chips - jnp.where(core == 1, odd, even), chips)
+        place = pl.ds(pl.multiple_of((2 * chip + (core ^ flip)) * cols, cols), cols)
         kv = dot(block, w_kv).astype(jnp.bfloat16).reshape(rows, cols, 2 * width)
         key_ref[:, place, :] = kv[:, :, :width]
         value_ref[:, place, :] = kv[:, :, width:]
@@ -137,11 +144,11 @@
     keys = panels[0].shape[1] // 2
     half = panels[0].shape[0]
     me = lax.axis_index("col")
-    p = [r[...] for r in panels]
+    p = [panels[(parts - k) % parts][...] for k in range(parts)]
     bit = 1
     while bit < parts:
-        flip = (me & bit) != 0
-        p = [jnp.where(flip, p[s ^ bit], p[s]) for s in range(parts)]
+        turn = (me & bit) != 0
+        p = [jnp.where(turn, p[(k - bit) % parts], p[k]) for k in range(parts)]
         bit *= 2
     for h in range(2):
         for c in range(0, parts, 2):
@@ -170,8 +177,25 @@
     out_ref[...] = result.astype(jnp.bfloat16).reshape(out_ref.shape)
 
 
-def swap(value, axis, size, distance):
-    return lax.ppermute(value, axis, [(i, i ^ distance) for i in range(size)])
+def swap(value, size):
+    return lax.ppermute(value, "row", [(i, i ^ 1) for i in range(size)])
+
+
+def chip_shift(value, size, odd, even):
+    pairs = [(i, (i + 2 * (odd if i % 2 else even)) % size) for i in range(size)]
+    return lax.ppermute(value, "row", pairs)
+
+
+def shift(value, axis, size, distance):
+    pairs = [(i, (i + distance) % size) for i in range(size)]
+    return lax.ppermute(value, axis, pairs)
+
+
+def row_plan(row_size):
+    shifts = list(reversed(range(1, row_size // 2)))
+    single = shifts[: len(shifts) % 2]
+    rest = shifts[len(single) :]
+    return single, [(rest[i], rest[i + 1]) for i in range(0, len(rest), 2)]
 
 
 def per_device(row_size, col_size, pair, group, w_query, w_key, w_value, w_gate, w_bias, w_out):
@@ -193,20 +217,28 @@
         + [pltpu.SemaphoreType.DMA((3,))],
         pltpu.HBM,
     )
-    blocks = {0: normed}
-    for s in range(2, row_size, 2):
-        blocks[s] = swap(normed, "row", row_size, s)
-    for s in range(0, row_size, 2):
-        blocks[s + 1] = swap(blocks[s], "row", row_size, 1)
-    panels = [panel] + [swap(panel, "col", col_size, s) for s in range(1, col_size)]
+    normed = normed[None]
+    sibling = swap(normed, row_size)
+    stacks, origins = [normed, sibling], [[(0, 0, 0)], [(1, 0, 0)]]
+    single, plan = row_plan(row_size)
+    for s in single:
+        arrived = chip_shift(normed, row_size, s, s)
+        stacks += [arrived, swap(arrived, row_size)]
+        origins += [[(0, s, s)], [(1, s, s)]]
+    both = jnp.concatenate([normed, sibling], axis=0)
+    for s, t in plan:
+        arrived = chip_shift(both, row_size, s, t)
+        stacks += [arrived, swap(arrived, row_size)]
+        origins += [[(0, s, t), (1, s, t)], [(1, t, s), (0, t, s)]]
+    panels = [panel] + [shift(panel, "col", col_size, s) for s in range(1, col_size)]
     scores, value, gate = call(
-        lambda *refs: scores_kernel(heads, row_size, *refs),
+        lambda *refs: scores_kernel(heads, origins, *refs),
         (
             shape((rows, cols * heads, all_keys), jnp.float32),
             shape((rows, all_keys, width), jnp.bfloat16),
             shape((rows, cols, width), jnp.float32),
         ),
-        [blocks[s] for s in range(row_size)] + [w_query, w_key, w_value, w_gate],
+        stacks + [w_query, w_key, w_value, w_gate],
         10**9,
         [pltpu.VMEM((rows, all_keys, width), jnp.bfloat16)],
     )

time: 22.9 us -> 21.1 us (0.921)
  waiting for transfers between devices: 9.75 us -> 6.87 us
  starting transfers between devices: 9 us -> 9.98 us
    ppermute x10 -> x8, waiting for transfers between devices: 9.75 us -> 6.87 us  [the longest x2 4.28 us: chip_shift(): return lax.ppermute(value, 'row', pairs)]
    ppermute x10 -> x8, starting transfers between devices: 9 us -> 9.98 us  [the longest x3 5.51 us: shift(): return lax.ppermute(value, axis, pairs)]
  transfers between devices with their start and end apart: 10 -> 8, of which waited for: 5 -> 4; matrix products, arithmetic and copies ran while one was open for 0% -> 0% of each run, Pallas kernels for 4% -> 4%
where the time goes in v1:
time: 21.1 us; the launch traced here: 20.9 us
  starting transfers between devices  9.98 us (47%)
  waiting for transfers between devices  6.87 us (33%)
  Pallas kernels  3.95 us (19%)
    ppermute x3, starting transfers between devices, shift(): return lax.ppermute(value, axis, pairs)  5.51 us
    ppermute x2, waiting for transfers between devices, chip_shift(): return lax.ppermute(value, 'row', pairs)  4.28 us
    pallas_call x3, Pallas kernels, call(): pl.pallas_call(kernel, out_shape=outs, in_specs=[pl.BlockSpec(memory_spac...  3.95 us
    ppermute x2, starting transfers between devices, chip_shift(): return lax.ppermute(value, 'row', pairs)  3.9 us
    ppermute x3, waiting for transfers between devices, shift(): return lax.ppermute(value, axis, pairs)  1.68 us
    ppermute x3, waiting for transfers between devices, swap(): return lax.ppermute(value, 'row', [(i, i ^ 1) for i in range(size)])  0.91 us
    ppermute x3, starting transfers between devices, swap(): return lax.ppermute(value, 'row', [(i, i ^ 1) for i in range(size)])  0.56 us
  transfers between devices with their start and end apart: 8, of which 4 were waited for; matrix products, arithmetic and copies ran while one was open for 0% of the time, Pallas kernels for 4%

profile of v1, /device:TPU:0, one launch (start us, length us, event | category | flops | bytes accessed | tf_op | source)
XLA Modules:
  0.0 20.9 jit_solution(736681887593680111)
XLA Ops:
  0.0 1.9 %shard_map.82 = (bf16[8,32,128]{2,1,0:T(8,128)(2,1)S(1)}, f32[64,128]{1,0:T(8,128)S(1)}) custom-call(bf16[8,32,128]{2,1,0:T(8,128)(2,1)} %refs_0_.1, bf16[32,64,128]{2,1,0:T(8,128)(2,1)} %refs_1_.1, f32[4,128]{1,0:T(4,128)} %bitcast.6), custom_call_target="tpu_custom_call" | custom-call | flops 2000000000 | bytes 1048576 | tf_op jit(solution)/shard_map/pallas_call | solution.py:18
  1.9 0.0 copy-start
  1.9 0.0 copy-start.1
  1.9 0.0 copy-start.2
  2.0 0.0 copy-start.3
  2.0 0.6 %collective-permute-start.3 = (bf16[1,8,32,128]{3,2,1,0:T(8,128)(2,1)S(1)}, bf16[1,8,32,128]{3,2,1,0:T(8,128)(2,1)S(1)}, u32[]{:S(2)}, u32[]{:S(2)}) collective-permute-start(bf16[1,8,32,128]{3,2,1,0:T(8,128)(2,1)S(1)} %bitcast.2), channel_id=1, source_target_pairs={{0,4},{4,0},{8,12},{12,8},{16,20},{20,16},{24,28},{28,24},{1,5},{5... | collective-permute-start | bytes 196616 | tf_op jit(solution)/shard_map/ppermute | solution.py:181
  2.5 0.9 %collective-permute-done.3.refs_1_ = bf16[1,8,32,128]{3,2,1,0:T(8,128)(2,1)S(1)} collective-permute-done((bf16[1,8,32,128]{3,2,1,0:T(8,128)(2,1)S(1)}, bf16[1,8,32,128]{3,2,1,0:T(8,128)(2,1)S(1)}, u32[]{:S(2)}, u32[]{:S(2)}) %collective-permute-start.3) | collective-permute-done | bytes 65568 | tf_op jit(solution)/shard_map/ppermute | solution.py:181
  3.5 2.9 %collective-permute-start.6 = (bf16[2,8,32,128]{3,2,1,0:T(8,128)(2,1)S(1)}, bf16[2,8,32,128]{3,2,1,0:T(8,128)(2,1)S(1)}, u32[]{:S(2)}, u32[]{:S(2)}) collective-permute-start(bf16[2,8,32,128]{3,2,1,0:T(8,128)(2,1)S(1)} %pad_maximum_fusion), channel_id=1, source_target_pairs={{0,8},{4,20},{8,16},{12,28},{16,24},{20,4},{24,0},{28,12},{1,9},{5... | collective-permute-start | bytes 393224 | tf_op jit(solution)/shard_map/ppermute | solution.py:186
  6.3 1.0 %collective-permute-start.4 = (bf16[1,8,32,128]{3,2,1,0:T(8,128)(2,1)S(1)}, bf16[1,8,32,128]{3,2,1,0:T(8,128)(2,1)S(1)}, u32[]{:S(2)}, u32[]{:S(2)}) collective-permute-start(bf16[1,8,32,128]{3,2,1,0:T(8,128)(2,1)S(1)} %bitcast.4), channel_id=1, source_target_pairs={{0,24},{4,28},{8,0},{12,4},{16,8},{20,12},{24,16},{28,20},{1,25},{... | collective-permute-start | bytes 196616 | tf_op jit(solution)/shard_map/ppermute | solution.py:186
  7.4 3.4 %collective-permute-done.6.refs_4_ = bf16[2,8,32,128]{3,2,1,0:T(8,128)(2,1)S(1)} collective-permute-done((bf16[2,8,32,128]{3,2,1,0:T(8,128)(2,1)S(1)}, bf16[2,8,32,128]{3,2,1,0:T(8,128)(2,1)S(1)}, u32[]{:S(2)}, u32[]{:S(2)}) %collective-permute-start.6) | collective-permute-done | bytes 131104 | tf_op jit(solution)/shard_map/ppermute | solution.py:186
  10.7 0.0 collective-permute-start.7
  10.7 0.9 %collective-permute-done.4.refs_2_ = bf16[1,8,32,128]{3,2,1,0:T(8,128)(2,1)S(1)} collective-permute-done((bf16[1,8,32,128]{3,2,1,0:T(8,128)(2,1)S(1)}, bf16[1,8,32,128]{3,2,1,0:T(8,128)(2,1)S(1)}, u32[]{:S(2)}, u32[]{:S(2)}) %collective-permute-start.4) | collective-permute-done | bytes 65568 | tf_op jit(solution)/shard_map/ppermute | solution.py:186
  11.6 0.0 collective-permute-start.5
  11.6 0.0 copy-start.4
  11.6 1.6 %collective-permute-start = (f32[64,128]{1,0:T(8,128)S(1)}, f32[64,128]{1,0:T(8,128)S(1)}, u32[]{:S(2)}, u32[]{:S(2)}) collective-permute-start(f32[64,128]{1,0:T(8,128)S(1)} %get-tuple-element.10.refs_0_), channel_id=1, source_target_pairs={{0,1},{1,2},{2,3},{3,0},{4,5},{5,6},{6,7},{7,4},{8,9},{9,10},{10,1... | collective-permute-start | bytes 98312 | tf_op jit(solution)/shard_map/ppermute | solution.py:191
  13.2 2.6 %collective-permute-start.1 = (f32[64,128]{1,0:T(8,128)S(1)}, f32[64,128]{1,0:T(8,128)S(1)}, u32[]{:S(2)}, u32[]{:S(2)}) collective-permute-start(f32[64,128]{1,0:T(8,128)S(1)} %get-tuple-element.10.refs_0_), channel_id=1, source_target_pairs={{0,2},{1,3},{2,0},{3,1},{4,6},{5,7},{6,4},{7,5},{8,10},{9,11},{10,... | collective-permute-start | bytes 98312 | tf_op jit(solution)/shard_map/ppermute | solution.py:191
  15.8 1.3 %collective-permute-start.2 = (f32[64,128]{1,0:T(8,128)S(1)}, f32[64,128]{1,0:T(8,128)S(1)}, u32[]{:S(2)}, u32[]{:S(2)}) collective-permute-start(f32[64,128]{1,0:T(8,128)S(1)} %get-tuple-element.10.refs_0_), channel_id=1, source_target_pairs={{0,3},{1,0},{2,1},{3,2},{4,7},{5,4},{6,5},{7,6},{8,11},{9,8},{10,9... | collective-permute-start | bytes 98312 | tf_op jit(solution)/shard_map/ppermute | solution.py:191
  17.2 0.0 collective-permute-done.5.refs_3_
  17.2 0.0 collective-permute-done.7.refs_5_
  17.2 0.0 copy-done
  17.2 0.0 copy-done.1
  17.2 0.0 copy-done.2
  17.2 0.0 copy-done.3
  17.2 0.8 %shard_map.83 = (f32[8,128,256]{2,1,0:T(8,128)S(1)}, bf16[8,256,128]{2,1,0:T(8,128)(2,1)S(1)}, f32[8,32,128]{2,1,0:T(8,128)S(1)}) custom-call(bf16[1,8,32,128]{3,2,1,0:T(8,128)(2,1)S(1)} %bitcast.5, bf16[1,8,32,128]{3,2,1,0:T(8,128)(2,1)S(1)} %collective-permute-done.3.refs_1_, bf16[1,8,32,128]{3,2,1,0:T(8,128)(2,1)S(1)} %collective-permute-done.4.refs_2_, ...), custom_call_target="tpu_custom_call" | custom-call | flops 1000000000 | bytes 1048576 | tf_op jit(solution)/shard_map/pallas_call | solution.py:18
  18.0 0.0 collective-permute-done.refs_1_
  18.0 0.0 collective-permute-done.1.refs_2_
  18.1 1.7 %collective-permute-done.2.refs_3_ = f32[64,128]{1,0:T(8,128)S(1)} collective-permute-done((f32[64,128]{1,0:T(8,128)S(1)}, f32[64,128]{1,0:T(8,128)S(1)}, u32[]{:S(2)}, u32[]{:S(2)}) %collective-permute-start.2) | collective-permute-done | bytes 32800 | tf_op jit(solution)/shard_map/ppermute | solution.py:191
  19.7 0.0 copy-done.4
  19.7 1.2 %shard_map.84 = bf16[8,32,128]{2,1,0:T(8,128)(2,1)} custom-call(f32[64,128]{1,0:T(8,128)S(1)} %get-tuple-element.10.refs_0_, f32[64,128]{1,0:T(8,128)S(1)} %collective-permute-done.refs_1_, f32[64,128]{1,0:T(8,128)S(1)} %collective-permute-done.1.refs_2_, f32[64,128]{1,0:T(8,128)S(1)} %collective-permute-done.2.refs_3_, ...), custom_call_target="tpu_custom_call" | custom-call | flops 1000000000 | bytes 1048576 | tf_op jit(solution)/shard_map/pallas_call | solution.py:18
  (1 shorter events, 0.0 us)
Async XLA Ops:
  1.9 15.2 %copy-start = (bf16[128,128]{1,0:T(8,128)(2,1)S(1)}, bf16[128,128]{1,0:T(8,128)(2,1)}, u32[]{:S(2)}) copy-start(bf16[128,128]{1,0:T(8,128)(2,1)} %refs_6_.1) | copy-start | bytes 98308
  1.9 15.2 %copy-start.1 = (bf16[128,128]{1,0:T(8,128)(2,1)S(1)}, bf16[128,128]{1,0:T(8,128)(2,1)}, u32[]{:S(2)}) copy-start(bf16[128,128]{1,0:T(8,128)(2,1)} %refs_7_.2) | copy-start | bytes 98308
  1.9 15.2 %copy-start.2 = (bf16[128,128]{1,0:T(8,128)(2,1)S(1)}, bf16[128,128]{1,0:T(8,128)(2,1)}, u32[]{:S(2)}) copy-start(bf16[128,128]{1,0:T(8,128)(2,1)} %refs_8_.1) | copy-start | bytes 98308
  2.0 15.2 %copy-start.3 = (bf16[128,128]{1,0:T(8,128)(2,1)S(1)}, bf16[128,128]{1,0:T(8,128)(2,1)}, u32[]{:S(2)}) copy-start(bf16[128,128]{1,0:T(8,128)(2,1)} %refs_9_.1) | copy-start | bytes 98308
  2.0 1.5 %collective-permute-start.3 = (bf16[1,8,32,128]{3,2,1,0:T(8,128)(2,1)S(1)}, bf16[1,8,32,128]{3,2,1,0:T(8,128)(2,1)S(1)}, u32[]{:S(2)}, u32[]{:S(2)}) collective-permute-start(bf16[1,8,32,128]{3,2,1,0:T(8,128)(2,1)S(1)} %bitcast.2), channel_id=1, source_target_pairs={{0,4},{4,0},{8,12},{12,8},{16,20},{20,16},{24,28},{28,24},{1,5},{5... | collective-permute-start | bytes 196616 | tf_op jit(solution)/shard_map/ppermute | solution.py:181
  3.5 7.3 %collective-permute-start.6 = (bf16[2,8,32,128]{3,2,1,0:T(8,128)(2,1)S(1)}, bf16[2,8,32,128]{3,2,1,0:T(8,128)(2,1)S(1)}, u32[]{:S(2)}, u32[]{:S(2)}) collective-permute-start(bf16[2,8,32,128]{3,2,1,0:T(8,128)(2,1)S(1)} %pad_maximum_fusion), channel_id=1, source_target_pairs={{0,8},{4,20},{8,16},{12,28},{16,24},{20,4},{24,0},{28,12},{1,9},{5... | collective-permute-start | bytes 393224 | tf_op jit(solution)/shard_map/ppermute | solution.py:186
  6.3 5.3 %collective-permute-start.4 = (bf16[1,8,32,128]{3,2,1,0:T(8,128)(2,1)S(1)}, bf16[1,8,32,128]{3,2,1,0:T(8,128)(2,1)S(1)}, u32[]{:S(2)}, u32[]{:S(2)}) collective-permute-start(bf16[1,8,32,128]{3,2,1,0:T(8,128)(2,1)S(1)} %bitcast.4), channel_id=1, source_target_pairs={{0,24},{4,28},{8,0},{12,4},{16,8},{20,12},{24,16},{28,20},{1,25},{... | collective-permute-start | bytes 196616 | tf_op jit(solution)/shard_map/ppermute | solution.py:186
  10.7 6.4 %collective-permute-start.7 = (bf16[2,8,32,128]{3,2,1,0:T(8,128)(2,1)S(1)}, bf16[2,8,32,128]{3,2,1,0:T(8,128)(2,1)S(1)}, u32[]{:S(2)}, u32[]{:S(2)}) collective-permute-start(bf16[2,8,32,128]{3,2,1,0:T(8,128)(2,1)S(1)} %collective-permute-done.6.refs_4_), channel_id=1, source_target_pairs={{0,4},{4,0},{8,12},{12,8},{16,20},{20,16},{24,28},{28,24},{1,5},{5... | collective-permute-start | bytes 393224 | tf_op jit(solution)/shard_map/ppermute | solution.py:181
  11.6 5.5 %collective-permute-start.5 = (bf16[1,8,32,128]{3,2,1,0:T(8,128)(2,1)S(1)}, bf16[1,8,32,128]{3,2,1,0:T(8,128)(2,1)S(1)}, u32[]{:S(2)}, u32[]{:S(2)}) collective-permute-start(bf16[1,8,32,128]{3,2,1,0:T(8,128)(2,1)S(1)} %collective-permute-done.4.refs_2_), channel_id=1, source_target_pairs={{0,4},{4,0},{8,12},{12,8},{16,20},{20,16},{24,28},{28,24},{1,5},{5... | collective-permute-start | bytes 196616 | tf_op jit(solution)/shard_map/ppermute | solution.py:181
  11.6 8.1 %copy-start.4 = (bf16[128,128]{1,0:T(8,128)(2,1)S(1)}, bf16[128,128]{1,0:T(8,128)(2,1)}, u32[]{:S(2)}) copy-start(bf16[128,128]{1,0:T(8,128)(2,1)} %refs_7_.3) | copy-start | bytes 98308
  11.6 6.4 %collective-permute-start = (f32[64,128]{1,0:T(8,128)S(1)}, f32[64,128]{1,0:T(8,128)S(1)}, u32[]{:S(2)}, u32[]{:S(2)}) collective-permute-start(f32[64,128]{1,0:T(8,128)S(1)} %get-tuple-element.10.refs_0_), channel_id=1, source_target_pairs={{0,1},{1,2},{2,3},{3,0},{4,5},{5,6},{6,7},{7,4},{8,9},{9,10},{10,1... | collective-permute-start | bytes 98312 | tf_op jit(solution)/shard_map/ppermute | solution.py:191
  13.2 4.8 %collective-permute-start.1 = (f32[64,128]{1,0:T(8,128)S(1)}, f32[64,128]{1,0:T(8,128)S(1)}, u32[]{:S(2)}, u32[]{:S(2)}) collective-permute-start(f32[64,128]{1,0:T(8,128)S(1)} %get-tuple-element.10.refs_0_), channel_id=1, source_target_pairs={{0,2},{1,3},{2,0},{3,1},{4,6},{5,7},{6,4},{7,5},{8,10},{9,11},{10,... | collective-permute-start | bytes 98312 | tf_op jit(solution)/shard_map/ppermute | solution.py:191
  15.8 3.9 %collective-permute-start.2 = (f32[64,128]{1,0:T(8,128)S(1)}, f32[64,128]{1,0:T(8,128)S(1)}, u32[]{:S(2)}, u32[]{:S(2)}) collective-permute-start(f32[64,128]{1,0:T(8,128)S(1)} %get-tuple-element.10.refs_0_), channel_id=1, source_target_pairs={{0,3},{1,0},{2,1},{3,2},{4,7},{5,4},{6,5},{7,6},{8,11},{9,8},{10,9... | collective-permute-start | bytes 98312 | tf_op jit(solution)/shard_map/ppermute | solution.py:191

commit v2 on v1

--- a/solution.py
+++ b/solution.py
@@ -14,13 +14,14 @@
 VMEM = pl.BlockSpec(memory_space=pltpu.VMEM)
 
 
-def call(kernel, outs, args, flops, scratch=(), space=pltpu.VMEM):
+def call(kernel, outs, args, flops, scratch=(), space=pltpu.VMEM, aliases=None):
     return pl.pallas_call(
         kernel,
         out_shape=outs,
         in_specs=[pl.BlockSpec(memory_space=space)] * len(args),
         out_specs=jax.tree.map(lambda _: VMEM, outs),
         scratch_shapes=list(scratch),
+        input_output_aliases=aliases or {},
         cost_estimate=pl.CostEstimate(flops=flops, bytes_accessed=1 << 20, transcendentals=0),
         compiler_params=pltpu.CompilerParams(vmem_limit_bytes=GRANT),
     )(*args)
@@ -35,22 +36,25 @@
     return high, value - high.astype(jnp.float32)
 
 
-def front_kernel(*refs):
-    sources, (normed_ref, out_ref), landed, semaphores = refs[:3], refs[3:5], refs[5:8], refs[8]
+def load_kernel(group_ref, pair_ref, w_ref, normed_ref, pair_out, w_out, landed, semaphores):
     copies = [
         pltpu.make_async_copy(a, b, semaphores.at[i])
-        for i, (a, b) in enumerate(zip(sources, landed))
+        for i, (a, b) in enumerate(
+            [(group_ref, landed), (pair_ref, pair_out), (w_ref, w_out)]
+        )
     ]
     for copy in copies:
         copy.start()
-    group_ref, pair_ref, w_ref = landed
     copies[0].wait()
-    rows = group_ref[...].astype(jnp.float32)
+    rows = landed[...].astype(jnp.float32)
     centered = rows - jnp.mean(rows, axis=-1, keepdims=True)
     spread = jnp.mean(centered * centered, axis=-1, keepdims=True)
     normed_ref[...] = (centered * lax.rsqrt(spread + EPS)).astype(jnp.bfloat16)
     copies[1].wait()
     copies[2].wait()
+
+
+def bias_kernel(pair_ref, w_ref, out_ref):
     cols, keys, channels = pair_ref.shape
     heads = w_ref.shape[0]
     half = cols // 2
@@ -98,31 +102,34 @@
             out_ref[pl.ds((at // 8) * 8 * heads + at % 8, heads, stride=8), :] = bias[0:heads]
 
 
-def scores_kernel(heads, origins, *refs):
-    sources = len(origins)
-    wq_ref, wk_ref, wv_ref, wg_ref, score_ref, value_ref, gate_ref, key_ref = refs[sources:]
-    _, rows, cols, channels = refs[0].shape
-    width = wq_ref.shape[1]
-    depth = width // heads
+def place_blocks(sources, origins, w_kv, key_ref, value_ref):
+    _, rows, cols, channels = sources[0].shape
+    width = value_ref.shape[2]
     me = lax.axis_index("row")
-    chips = key_ref.shape[1] // (2 * cols)
-    own = refs[0][0].reshape(rows * cols, channels)
-    both = dot(own, jnp.concatenate([wq_ref[...], wg_ref[...]], axis=1))
-    gate_ref[...] = jax.nn.sigmoid(both[:, width:]).reshape(rows, cols, width)
-    query = both[:, :width] * (1.0 / math.sqrt(depth))
-    w_kv = jnp.concatenate([wk_ref[...], wv_ref[...]], axis=1)
     for ref, entry, (flip, odd, even) in [
         (ref, entry, origin)
-        for ref, group in zip(refs, origins)
+        for ref, group in zip(sources, origins)
         for entry, origin in enumerate(group)
     ]:
         block = ref[entry].reshape(rows * cols, channels)
         core = me & 1
-        chip = lax.rem((me >> 1) + chips - jnp.where(core == 1, odd, even), chips)
+        chip = (me >> 1) ^ jnp.where(core == 1, odd, even)
         place = pl.ds(pl.multiple_of((2 * chip + (core ^ flip)) * cols, cols), cols)
         kv = dot(block, w_kv).astype(jnp.bfloat16).reshape(rows, cols, 2 * width)
         key_ref[:, place, :] = kv[:, :, :width]
         value_ref[:, place, :] = kv[:, :, width:]
+
+
+def early_kernel(heads, origins, *refs):
+    sources = refs[: len(origins)]
+    wq_ref, wk_ref, wv_ref, wg_ref, key_ref, value_ref, gate_ref, stack_ref = refs[len(origins) :]
+    _, rows, cols, channels = sources[0].shape
+    width = wq_ref.shape[1]
+    depth = width // heads
+    own = sources[0][0].reshape(rows * cols, channels)
+    both = dot(own, jnp.concatenate([wq_ref[...], wg_ref[...]], axis=1))
+    gate_ref[...] = jax.nn.sigmoid(both[:, width:]).reshape(rows, cols, width)
+    query = both[:, :width] * (1.0 / math.sqrt(depth))
     lane = lax.broadcasted_iota(jnp.int32, (8, width), 1) // depth
     for row in range(rows):
         tiles = []
@@ -130,25 +137,43 @@
             tile = query[row * cols + g * 8 : row * cols + g * 8 + 8]
             for h in range(heads):
                 tiles.append(jnp.where(lane == h, tile, 0.0))
-        stacked = jnp.concatenate(tiles, axis=0).astype(jnp.bfloat16)
+        stack_ref[row] = jnp.concatenate(tiles, axis=0).astype(jnp.bfloat16)
+    w_kv = jnp.concatenate([wk_ref[...], wv_ref[...]], axis=1)
+    place_blocks(sources, origins, w_kv, key_ref, value_ref)
+
+
+def scores_kernel(origins, *refs):
+    sources = refs[: len(origins)]
+    stack_ref, wk_ref, wv_ref, _, _, score_ref, key_ref, value_ref = refs[len(origins) :]
+    w_kv = jnp.concatenate([wk_ref[...], wv_ref[...]], axis=1)
+    place_blocks(sources, origins, w_kv, key_ref, value_ref)
+    for row in range(stack_ref.shape[0]):
         score_ref[row] = lax.dot_general(
-            stacked, key_ref[row], NT, preferred_element_type=jnp.float32
+            stack_ref[row], key_ref[row], NT, preferred_element_type=jnp.float32
         )
 
 
-def attention_kernel(heads, parts, *refs):
-    panels = refs[:parts]
-    score_ref, value_ref, gate_ref, wo_ref, out_ref, bias_ref, hidden_ref = refs[parts:]
+def attention_kernel(heads, single, plan, *refs):
+    sources = 1 + len(single) + 2 * len(plan)
+    score_ref, value_ref, gate_ref, wo_ref, out_ref, bias_ref, hidden_ref = refs[sources:]
     rows, cols, width = gate_ref.shape
     depth = width // heads
-    keys = panels[0].shape[1] // 2
-    half = panels[0].shape[0]
+    half, keys = refs[0].shape[0], refs[0].shape[1] // 2
+    odd = (lax.axis_index("row") & 1) == 1
     me = lax.axis_index("col")
-    p = [panels[(parts - k) % parts][...] for k in range(parts)]
+    parts = sources
+    p = [refs[0][...]] + [None] * (parts - 1)
+    for at, s in enumerate(single):
+        p[s] = refs[1 + at][...]
+    for at, (s, t) in enumerate(plan):
+        arrived = refs[1 + len(single) + 2 * at][:half]
+        passed = refs[2 + len(single) + 2 * at][half:]
+        p[s] = jnp.where(odd, arrived, passed)
+        p[t] = jnp.where(odd, passed, arrived)
     bit = 1
     while bit < parts:
         turn = (me & bit) != 0
-        p = [jnp.where(turn, p[(k - bit) % parts], p[k]) for k in range(parts)]
+        p = [jnp.where(turn, p[k ^ bit], p[k]) for k in range(parts)]
         bit *= 2
     for h in range(2):
         for c in range(0, parts, 2):
@@ -182,20 +207,30 @@
 
 
 def chip_shift(value, size, odd, even):
-    pairs = [(i, (i + 2 * (odd if i % 2 else even)) % size) for i in range(size)]
+    pairs = [(i, i ^ (2 * (odd if i % 2 else even))) for i in range(size)]
     return lax.ppermute(value, "row", pairs)
 
 
-def shift(value, axis, size, distance):
-    pairs = [(i, (i + distance) % size) for i in range(size)]
-    return lax.ppermute(value, axis, pairs)
+def col_shift(value, row_size, col_size, odd, even):
+    pairs = [
+        (r * col_size + c, r * col_size + (c ^ (odd if r % 2 else even)))
+        for r in range(row_size)
+        for c in range(col_size)
+    ]
+    return lax.ppermute(value, ("row", "col"), pairs)
+
+
+def pair_up(distances):
+    return [tuple(distances[i : i + 2]) for i in range(0, len(distances), 2)]
 
 
 def row_plan(row_size):
-    shifts = list(reversed(range(1, row_size // 2)))
-    single = shifts[: len(shifts) % 2]
-    rest = shifts[len(single) :]
-    return single, [(rest[i], rest[i + 1]) for i in range(0, len(rest), 2)]
+    chips = row_size // 2
+    return [chips - 1], pair_up(list(range(1, chips - 1)))
+
+
+def col_plan(col_size):
+    return [1], pair_up(list(reversed(range(2, col_size))))
 
 
 def per_device(row_size, col_size, pair, group, w_query, w_key, w_value, w_gate, w_bias, w_out):
@@ -205,17 +240,21 @@
     keys = pair.shape[1]
     all_keys = row_size * cols
     shape = jax.ShapeDtypeStruct
-    normed, panel = call(
-        front_kernel,
+    inputs = [pltpu.with_memory_space_constraint(a, pltpu.HBM) for a in (group, pair, w_bias.T)]
+    normed, pair, w_bias = call(
+        load_kernel,
         (
             shape(group.shape, jnp.bfloat16),
-            shape((cols * heads // 2, 2 * keys), jnp.float32),
+            shape(pair.shape, pair.dtype),
+            shape(inputs[2].shape, jnp.float32),
         ),
-        [pltpu.with_memory_space_constraint(a, pltpu.HBM) for a in (group, pair, w_bias.T)],
-        2 * 10**9,
-        [pltpu.VMEM(a.shape, a.dtype) for a in (group, pair, w_bias.T)]
-        + [pltpu.SemaphoreType.DMA((3,))],
+        inputs,
+        10**8,
+        [pltpu.VMEM(group.shape, group.dtype), pltpu.SemaphoreType.DMA((3,))],
         pltpu.HBM,
+    )
+    panel = call(
+        bias_kernel, shape((cols * heads // 2, 2 * keys), jnp.float32), [pair, w_bias], 2 * 10**9
     )
     normed = normed[None]
     sibling = swap(normed, row_size)
@@ -230,20 +269,38 @@
         arrived = chip_shift(both, row_size, s, t)
         stacks += [arrived, swap(arrived, row_size)]
         origins += [[(0, s, t), (1, s, t)], [(1, t, s), (0, t, s)]]
-    panels = [panel] + [shift(panel, "col", col_size, s) for s in range(1, col_size)]
-    scores, value, gate = call(
-        lambda *refs: scores_kernel(heads, origins, *refs),
+    near, distant = col_plan(col_size)
+    panels = [panel]
+    for s in near:
+        panels.append(col_shift(panel, row_size, col_size, s, s))
+    both = jnp.concatenate([panel, swap(panel, row_size)], axis=0)
+    for s, t in distant:
+        arrived = col_shift(both, row_size, col_size, s, t)
+        panels += [arrived, swap(arrived, row_size)]
+    keys_shape = shape((rows, all_keys, width), jnp.bfloat16)
+    soon = [0, 1] + list(range(2, len(stacks), 2))
+    late = list(range(3, len(stacks), 2))
+    key, value, gate, queries = call(
+        lambda *refs: early_kernel(heads, [origins[i] for i in soon], *refs),
         (
-            shape((rows, cols * heads, all_keys), jnp.float32),
-            shape((rows, all_keys, width), jnp.bfloat16),
+            keys_shape,
+            keys_shape,
             shape((rows, cols, width), jnp.float32),
+            shape((rows, cols * heads, width), jnp.bfloat16),
         ),
-        stacks + [w_query, w_key, w_value, w_gate],
+        [stacks[i] for i in soon] + [w_query, w_key, w_value, w_gate],
         10**9,
-        [pltpu.VMEM((rows, all_keys, width), jnp.bfloat16)],
+    )
+    late_args = [stacks[i] for i in late] + [queries, w_key, w_value, key, value]
+    scores, _, value = call(
+        lambda *refs: scores_kernel([origins[i] for i in late], *refs),
+        (shape((rows, cols * heads, all_keys), jnp.float32), keys_shape, keys_shape),
+        late_args,
+        10**9,
+        aliases={len(late_args) - 2: 1, len(late_args) - 1: 2},
     )
     return call(
-        lambda *refs: attention_kernel(heads, col_size, *refs),
+        lambda *refs: attention_kernel(heads, near, distant, *refs),
         shape((rows, cols, w_out.shape[1]), jnp.bfloat16),
         panels + [scores, value, gate, w_out],
         10**9,

time: 21.1 us -> 16.6 us (0.79)
  waiting for transfers between devices: 6.87 us -> 2.93 us
  starting transfers between devices: 9.98 us -> 9.25 us
    ppermute x2, waiting for transfers between devices: 4.28 us -> 1.46 us  [chip_shift(): return lax.ppermute(value, 'row', pairs)]
    ppermute x3 -> x2, starting transfers between devices: 5.51 us -> 4.16 us  [col_shift(): return lax.ppermute(value, ('row', 'col'), pairs)]
    ppermute x3 -> x2, waiting for transfers between devices: 1.68 us -> 1.05 us  [col_shift(): return lax.ppermute(value, ('row', 'col'), pairs)]
    ppermute x3 -> x5, waiting for transfers between devices: 0.91 us -> 0.42 us  [swap(): return lax.ppermute(value, 'row', [(i, i ^ 1) for i in range(size)])]
    ppermute x3 -> x5, starting transfers between devices: 0.56 us -> 1.01 us  [swap(): return lax.ppermute(value, 'row', [(i, i ^ 1) for i in range(size)])]
    pallas_call x3 -> x5, Pallas kernels: 3.95 us -> 4.08 us  [call(): pl.pallas_call(kernel, out_shape=outs, in_specs=[pl.BlockSpec(memory_spac...]
  transfers between devices with their start and end apart: 8 -> 9, of which waited for: 4 -> 4; matrix products, arithmetic and copies ran while one was open for 0% -> 0% of each run, Pallas kernels for 4% -> 11%
where the time goes in v2:
time: 16.6 us; the launch traced here: 16.4 us
  starting transfers between devices  9.25 us (56%)
  Pallas kernels  4.08 us (25%)
  waiting for transfers between devices  2.93 us (18%)
    ppermute x2, starting transfers between devices, col_shift(): return lax.ppermute(value, ('row', 'col'), pairs)  4.16 us
    ppermute x2, starting transfers between devices, chip_shift(): return lax.ppermute(value, 'row', pairs)  4.08 us
    pallas_call x5, Pallas kernels, call(): pl.pallas_call(kernel, out_shape=outs, in_specs=[pl.BlockSpec(memory_spac...  4.08 us
    ppermute x2, waiting for transfers between devices, chip_shift(): return lax.ppermute(value, 'row', pairs)  1.46 us
    ppermute x2, waiting for transfers between devices, col_shift(): return lax.ppermute(value, ('row', 'col'), pairs)  1.05 us
    ppermute x5, starting transfers between devices, swap(): return lax.ppermute(value, 'row', [(i, i ^ 1) for i in range(size)])  1.01 us
    ppermute x5, waiting for transfers between devices, swap(): return lax.ppermute(value, 'row', [(i, i ^ 1) for i in range(size)])  0.42 us
  transfers between devices with their start and end apart: 9, of which 4 were waited for; matrix products, arithmetic and copies ran while one was open for 0% of the time, Pallas kernels for 11%

profile of v2, /device:TPU:0, one launch (start us, length us, event | category | flops | bytes accessed | tf_op | source)
XLA Modules:
  0.0 16.4 jit_solution(16742784052719740322)
XLA Ops:
  0.0 1.1 %shard_map.82 = (bf16[8,32,128]{2,1,0:T(8,128)(2,1)S(1)}, bf16[32,64,128]{2,1,0:T(8,128)(2,1)S(1)}, f32[4,128]{1,0:T(4,128)S(1)}) custom-call(bf16[8,32,128]{2,1,0:T(8,128)(2,1)} %group_ref.1, bf16[32,64,128]{2,1,0:T(8,128)(2,1)} %pair_ref.1, f32[4,128]{1,0:T(4,128)} %bitcast.6), custom_call_target="tpu_custom_call" | custom-call | flops 100000000 | bytes 1048576 | tf_op jit(solution)/shard_map/pallas_call | solution.py:18
  1.1 0.6 %collective-permute-start.6 = (bf16[1,8,32,128]{3,2,1,0:T(8,128)(2,1)S(1)}, bf16[1,8,32,128]{3,2,1,0:T(8,128)(2,1)S(1)}, u32[]{:S(2)}, u32[]{:S(2)}) collective-permute-start(bf16[1,8,32,128]{3,2,1,0:T(8,128)(2,1)S(1)} %bitcast.2), channel_id=1, source_target_pairs={{0,4},{4,0},{8,12},{12,8},{16,20},{20,16},{24,28},{28,24},{1,5},{5... | collective-permute-start | bytes 196616 | tf_op jit(solution)/shard_map/ppermute | solution.py:206
  1.7 3.5 %collective-permute-start.4 = (bf16[1,8,32,128]{3,2,1,0:T(8,128)(2,1)S(1)}, bf16[1,8,32,128]{3,2,1,0:T(8,128)(2,1)S(1)}, u32[]{:S(2)}, u32[]{:S(2)}) collective-permute-start(bf16[1,8,32,128]{3,2,1,0:T(8,128)(2,1)S(1)} %bitcast.3), channel_id=1, source_target_pairs={{0,24},{4,28},{8,16},{12,20},{16,8},{20,12},{24,0},{28,4},{1,25},{... | collective-permute-start | bytes 196616 | tf_op jit(solution)/shard_map/ppermute | solution.py:211
  5.2 0.8 %shard_map.83.refs_0_ = f32[64,128]{1,0:T(8,128)S(1)} custom-call(bf16[32,64,128]{2,1,0:T(8,128)(2,1)S(1)} %get-tuple-element.14.pair_ref, f32[4,128]{1,0:T(4,128)S(1)} %get-tuple-element.15.w_ref), custom_call_target="tpu_custom_call" | custom-call | flops 2000000000 | bytes 1048576 | tf_op jit(solution)/shard_map/pallas_call | solution.py:18
  6.0 0.2 %collective-permute-start.1 = (f32[64,128]{1,0:T(8,128)S(1)}, f32[64,128]{1,0:T(8,128)S(1)}, u32[]{:S(2)}, u32[]{:S(2)}) collective-permute-start(f32[64,128]{1,0:T(8,128)S(1)} %shard_map.83.refs_0_), channel_id=1, source_target_pairs={{0,4},{4,0},{8,12},{12,8},{16,20},{20,16},{24,28},{28,24},{1,5},{5... | collective-permute-start | bytes 98312 | tf_op jit(solution)/shard_map/ppermute | solution.py:206
  6.2 0.0 collective-permute-done.6.refs_1_
  6.2 0.0 copy-start
  6.2 0.0 copy-start.1
  6.2 0.0 copy-start.2
  6.3 0.0 copy-start.3
  6.3 0.6 %collective-permute-start.7 = (bf16[2,8,32,128]{3,2,1,0:T(8,128)(2,1)S(1)}, bf16[2,8,32,128]{3,2,1,0:T(8,128)(2,1)S(1)}, u32[]{:S(2)}, u32[]{:S(2)}) collective-permute-start(bf16[2,8,32,128]{3,2,1,0:T(8,128)(2,1)S(1)} %pad_maximum_fusion), channel_id=1, source_target_pairs={{0,16},{4,12},{8,24},{12,4},{16,0},{20,28},{24,8},{28,20},{1,17},{... | collective-permute-start | bytes 393224 | tf_op jit(solution)/shard_map/ppermute | solution.py:211
  6.8 0.4 %collective-permute-done.1 = f32[64,128]{1,0:T(8,128)S(1)} collective-permute-done((f32[64,128]{1,0:T(8,128)S(1)}, f32[64,128]{1,0:T(8,128)S(1)}, u32[]{:S(2)}, u32[]{:S(2)}) %collective-permute-start.1) | collective-permute-done | bytes 32800 | tf_op jit(solution)/shard_map/ppermute | solution.py:206
  7.3 2.6 %collective-permute-start.2 = (f32[128,128]{1,0:T(8,128)S(1)}, f32[128,128]{1,0:T(8,128)S(1)}, u32[]{:S(2)}, u32[]{:S(2)}) collective-permute-start(f32[128,128]{1,0:T(8,128)S(1)} %pad_maximum_fusion.1), channel_id=1, source_target_pairs={{0,2},{1,3},{2,0},{3,1},{4,7},{5,6},{6,5},{7,4},{8,10},{9,11},{10,... | collective-permute-start | bytes 196616 | tf_op jit(solution)/shard_map/ppermute | solution.py:220
  9.8 1.5 %collective-permute-done.7.refs_3_ = bf16[2,8,32,128]{3,2,1,0:T(8,128)(2,1)S(1)} collective-permute-done((bf16[2,8,32,128]{3,2,1,0:T(8,128)(2,1)S(1)}, bf16[2,8,32,128]{3,2,1,0:T(8,128)(2,1)S(1)}, u32[]{:S(2)}, u32[]{:S(2)}) %collective-permute-start.7) | collective-permute-done | bytes 131104 | tf_op jit(solution)/shard_map/ppermute | solution.py:211
  11.3 0.0 collective-permute-start.8
  11.3 1.6 %collective-permute-start = (f32[64,128]{1,0:T(8,128)S(1)}, f32[64,128]{1,0:T(8,128)S(1)}, u32[]{:S(2)}, u32[]{:S(2)}) collective-permute-start(f32[64,128]{1,0:T(8,128)S(1)} %shard_map.83.refs_0_), channel_id=1, source_target_pairs={{0,1},{1,0},{2,3},{3,2},{4,5},{5,4},{6,7},{7,6},{8,9},{9,8},{10,11... | collective-permute-start | bytes 98312 | tf_op jit(solution)/shard_map/ppermute | solution.py:220
  12.9 0.0 collective-permute-done.4.refs_2_
  12.9 0.2 %collective-permute-start.5 = (bf16[1,8,32,128]{3,2,1,0:T(8,128)(2,1)S(1)}, bf16[1,8,32,128]{3,2,1,0:T(8,128)(2,1)S(1)}, u32[]{:S(2)}, u32[]{:S(2)}) collective-permute-start(bf16[1,8,32,128]{3,2,1,0:T(8,128)(2,1)S(1)} %collective-permute-done.4.refs_2_), channel_id=1, source_target_pairs={{0,4},{4,0},{8,12},{12,8},{16,20},{20,16},{24,28},{28,24},{1,5},{5... | collective-permute-start | bytes 196616 | tf_op jit(solution)/shard_map/ppermute | solution.py:206
  13.1 0.7 %collective-permute-done.2.refs_2_ = f32[128,128]{1,0:T(8,128)S(1)} collective-permute-done((f32[128,128]{1,0:T(8,128)S(1)}, f32[128,128]{1,0:T(8,128)S(1)}, u32[]{:S(2)}, u32[]{:S(2)}) %collective-permute-start.2) | collective-permute-done | bytes 65568 | tf_op jit(solution)/shard_map/ppermute | solution.py:220
  13.8 0.0 collective-permute-start.3
  13.8 0.0 copy-done
  13.8 0.0 copy-done.1
  13.8 0.0 copy-done.2
  13.9 0.0 copy-done.3
  13.9 0.4 %shard_map.84 = (bf16[8,256,128]{2,1,0:T(8,128)(2,1)S(1)}, bf16[8,256,128]{2,1,0:T(8,128)(2,1)S(1)}, f32[8,32,128]{2,1,0:T(8,128)S(1)}, bf16[8,128,128]{2,1,0:T(8,128)(2,1)S(1)}) custom-call(bf16[1,8,32,128]{3,2,1,0:T(8,128)(2,1)S(1)} %bitcast.5, bf16[1,8,32,128]{3,2,1,0:T(8,128)(2,1)S(1)} %collective-permute-done.6.refs_1_, ...), custom_call_target="tpu_custom_call" | custom-call | flops 1000000000 | bytes 1048576 | tf_op jit(solution)/shard_map/pallas_call | solution.py:18
  14.2 0.0 collective-permute-done.5.refs_0_
  14.2 0.0 collective-permute-done.8.refs_1_
  14.3 0.0 copy-start.4
  14.3 0.6 %shard_map.85 = (f32[8,128,256]{2,1,0:T(8,128)S(1)}, bf16[8,256,128]{2,1,0:T(8,128)(2,1)S(1)}, bf16[8,256,128]{2,1,0:T(8,128)(2,1)S(1)}) custom-call(bf16[1,8,32,128]{3,2,1,0:T(8,128)(2,1)S(1)} %collective-permute-done.5.refs_0_, bf16[2,8,32,128]{3,2,1,0:T(8,128)(2,1)S(1)} %collective-permute-done.8.refs_1_, ...), custom_call_target="tpu_custom_call", output_to_operand_aliasing={{1}: (5, {}), {2}: (6, {})} | custom-call | flops 1000000000 | bytes 1048576 | tf_op jit(solution)/shard_map/pallas_call | solution.py:18
  14.9 0.3 %collective-permute-done.refs_1_ = f32[64,128]{1,0:T(8,128)S(1)} collective-permute-done((f32[64,128]{1,0:T(8,128)S(1)}, f32[64,128]{1,0:T(8,128)S(1)}, u32[]{:S(2)}, u32[]{:S(2)}) %collective-permute-start) | collective-permute-done | bytes 32800 | tf_op jit(solution)/shard_map/ppermute | solution.py:220
  15.2 0.0 collective-permute-done.3.refs_3_
  15.2 0.0 copy-done.4
  15.2 1.2 %shard_map.86 = bf16[8,32,128]{2,1,0:T(8,128)(2,1)} custom-call(f32[64,128]{1,0:T(8,128)S(1)} %shard_map.83.refs_0_, f32[64,128]{1,0:T(8,128)S(1)} %collective-permute-done.refs_1_, f32[128,128]{1,0:T(8,128)S(1)} %collective-permute-done.2.refs_2_, f32[128,128]{1,0:T(8,128)S(1)} %collective-permute-done.3.refs_3_, ...), custom_call_target="tpu_custom_call" | custom-call | flops 1000000000 | bytes 1048576 | tf_op jit(solution)/shard_map/pallas_call | solution.py:18
  (2 shorter events, 0.0 us)
Async XLA Ops:
  1.1 5.1 %collective-permute-start.6 = (bf16[1,8,32,128]{3,2,1,0:T(8,128)(2,1)S(1)}, bf16[1,8,32,128]{3,2,1,0:T(8,128)(2,1)S(1)}, u32[]{:S(2)}, u32[]{:S(2)}) collective-permute-start(bf16[1,8,32,128]{3,2,1,0:T(8,128)(2,1)S(1)} %bitcast.2), channel_id=1, source_target_pairs={{0,4},{4,0},{8,12},{12,8},{16,20},{20,16},{24,28},{28,24},{1,5},{5... | collective-permute-start | bytes 196616 | tf_op jit(solution)/shard_map/ppermute | solution.py:206
  1.7 11.2 %collective-permute-start.4 = (bf16[1,8,32,128]{3,2,1,0:T(8,128)(2,1)S(1)}, bf16[1,8,32,128]{3,2,1,0:T(8,128)(2,1)S(1)}, u32[]{:S(2)}, u32[]{:S(2)}) collective-permute-start(bf16[1,8,32,128]{3,2,1,0:T(8,128)(2,1)S(1)} %bitcast.3), channel_id=1, source_target_pairs={{0,24},{4,28},{8,16},{12,20},{16,8},{20,12},{24,0},{28,4},{1,25},{... | collective-permute-start | bytes 196616 | tf_op jit(solution)/shard_map/ppermute | solution.py:211
  6.0 1.3 %collective-permute-start.1 = (f32[64,128]{1,0:T(8,128)S(1)}, f32[64,128]{1,0:T(8,128)S(1)}, u32[]{:S(2)}, u32[]{:S(2)}) collective-permute-start(f32[64,128]{1,0:T(8,128)S(1)} %shard_map.83.refs_0_), channel_id=1, source_target_pairs={{0,4},{4,0},{8,12},{12,8},{16,20},{20,16},{24,28},{28,24},{1,5},{5... | collective-permute-start | bytes 98312 | tf_op jit(solution)/shard_map/ppermute | solution.py:206
  6.2 7.6 %copy-start = (bf16[128,128]{1,0:T(8,128)(2,1)S(1)}, bf16[128,128]{1,0:T(8,128)(2,1)}, u32[]{:S(2)}) copy-start(bf16[128,128]{1,0:T(8,128)(2,1)} %refs_4_.2) | copy-start | bytes 98308
  6.2 7.6 %copy-start.1 = (bf16[128,128]{1,0:T(8,128)(2,1)S(1)}, bf16[128,128]{1,0:T(8,128)(2,1)}, u32[]{:S(2)}) copy-start(bf16[128,128]{1,0:T(8,128)(2,1)} %refs_7_.2) | copy-start | bytes 98308
  6.2 7.6 %copy-start.2 = (bf16[128,128]{1,0:T(8,128)(2,1)S(1)}, bf16[128,128]{1,0:T(8,128)(2,1)}, u32[]{:S(2)}) copy-start(bf16[128,128]{1,0:T(8,128)(2,1)} %refs_3_.1) | copy-start | bytes 98308
  6.3 7.6 %copy-start.3 = (bf16[128,128]{1,0:T(8,128)(2,1)S(1)}, bf16[128,128]{1,0:T(8,128)(2,1)}, u32[]{:S(2)}) copy-start(bf16[128,128]{1,0:T(8,128)(2,1)} %refs_4_.3) | copy-start | bytes 98308
  6.3 5.0 %collective-permute-start.7 = (bf16[2,8,32,128]{3,2,1,0:T(8,128)(2,1)S(1)}, bf16[2,8,32,128]{3,2,1,0:T(8,128)(2,1)S(1)}, u32[]{:S(2)}, u32[]{:S(2)}) collective-permute-start(bf16[2,8,32,128]{3,2,1,0:T(8,128)(2,1)S(1)} %pad_maximum_fusion), channel_id=1, source_target_pairs={{0,16},{4,12},{8,24},{12,4},{16,0},{20,28},{24,8},{28,20},{1,17},{... | collective-permute-start | bytes 393224 | tf_op jit(solution)/shard_map/ppermute | solution.py:211
  7.3 6.6 %collective-permute-start.2 = (f32[128,128]{1,0:T(8,128)S(1)}, f32[128,128]{1,0:T(8,128)S(1)}, u32[]{:S(2)}, u32[]{:S(2)}) collective-permute-start(f32[128,128]{1,0:T(8,128)S(1)} %pad_maximum_fusion.1), channel_id=1, source_target_pairs={{0,2},{1,3},{2,0},{3,1},{4,7},{5,6},{6,5},{7,4},{8,10},{9,11},{10,... | collective-permute-start | bytes 196616 | tf_op jit(solution)/shard_map/ppermute | solution.py:220
  11.3 2.9 %collective-permute-start.8 = (bf16[2,8,32,128]{3,2,1,0:T(8,128)(2,1)S(1)}, bf16[2,8,32,128]{3,2,1,0:T(8,128)(2,1)S(1)}, u32[]{:S(2)}, u32[]{:S(2)}) collective-permute-start(bf16[2,8,32,128]{3,2,1,0:T(8,128)(2,1)S(1)} %collective-permute-done.7.refs_3_), channel_id=1, source_target_pairs={{0,4},{4,0},{8,12},{12,8},{16,20},{20,16},{24,28},{28,24},{1,5},{5... | collective-permute-start | bytes 393224 | tf_op jit(solution)/shard_map/ppermute | solution.py:206
  11.3 3.9 %collective-permute-start = (f32[64,128]{1,0:T(8,128)S(1)}, f32[64,128]{1,0:T(8,128)S(1)}, u32[]{:S(2)}, u32[]{:S(2)}) collective-permute-start(f32[64,128]{1,0:T(8,128)S(1)} %shard_map.83.refs_0_), channel_id=1, source_target_pairs={{0,1},{1,0},{2,3},{3,2},{4,5},{5,4},{6,7},{7,6},{8,9},{9,8},{10,11... | collective-permute-start | bytes 98312 | tf_op jit(solution)/shard_map/ppermute | solution.py:220
  12.9 1.3 %collective-permute-start.5 = (bf16[1,8,32,128]{3,2,1,0:T(8,128)(2,1)S(1)}, bf16[1,8,32,128]{3,2,1,0:T(8,128)(2,1)S(1)}, u32[]{:S(2)}, u32[]{:S(2)}) collective-permute-start(bf16[1,8,32,128]{3,2,1,0:T(8,128)(2,1)S(1)} %collective-permute-done.4.refs_2_), channel_id=1, source_target_pairs={{0,4},{4,0},{8,12},{12,8},{16,20},{20,16},{24,28},{28,24},{1,5},{5... | collective-permute-start | bytes 196616 | tf_op jit(solution)/shard_map/ppermute | solution.py:206
  13.8 1.4 %collective-permute-start.3 = (f32[128,128]{1,0:T(8,128)S(1)}, f32[128,128]{1,0:T(8,128)S(1)}, u32[]{:S(2)}, u32[]{:S(2)}) collective-permute-start(f32[128,128]{1,0:T(8,128)S(1)} %collective-permute-done.2.refs_2_), channel_id=1, source_target_pairs={{0,4},{4,0},{8,12},{12,8},{16,20},{20,16},{24,28},{28,24},{1,5},{5... | collective-permute-start | bytes 196616 | tf_op jit(solution)/shard_map/ppermute | solution.py:206
  14.3 1.0 %copy-start.4 = (bf16[128,128]{1,0:T(8,128)(2,1)S(1)}, bf16[128,128]{1,0:T(8,128)(2,1)}, u32[]{:S(2)}) copy-start(bf16[128,128]{1,0:T(8,128)(2,1)} %refs_7_.3) | copy-start | bytes 98308

commit v3 on v2

--- a/solution.py
+++ b/solution.py
@@ -11,6 +11,7 @@
 EPS = 1e-05
 NT = (((1,), (1,)), ((), ()))
 GRANT = 16 << 20
+HINT = 10**10
 VMEM = pl.BlockSpec(memory_space=pltpu.VMEM)
 
 
@@ -36,25 +37,25 @@
     return high, value - high.astype(jnp.float32)
 
 
-def load_kernel(group_ref, pair_ref, w_ref, normed_ref, pair_out, w_out, landed, semaphores):
-    copies = [
-        pltpu.make_async_copy(a, b, semaphores.at[i])
-        for i, (a, b) in enumerate(
-            [(group_ref, landed), (pair_ref, pair_out), (w_ref, w_out)]
-        )
-    ]
-    for copy in copies:
-        copy.start()
-    copies[0].wait()
-    rows = landed[...].astype(jnp.float32)
+def normalize(rows):
+    rows = rows.astype(jnp.float32)
     centered = rows - jnp.mean(rows, axis=-1, keepdims=True)
     spread = jnp.mean(centered * centered, axis=-1, keepdims=True)
-    normed_ref[...] = (centered * lax.rsqrt(spread + EPS)).astype(jnp.bfloat16)
-    copies[1].wait()
-    copies[2].wait()
-
-
-def bias_kernel(pair_ref, w_ref, out_ref):
+    return (centered * lax.rsqrt(spread + EPS)).astype(jnp.bfloat16)
+
+
+def seed_kernel(averages_ref):
+    channels = averages_ref.shape[0] // 2
+    even = jnp.full((channels, channels), 1.0 / channels, jnp.bfloat16)
+    blank = jnp.zeros((channels, channels), jnp.bfloat16)
+    averages_ref[...] = jnp.concatenate(
+        [jnp.concatenate([even, blank], axis=1), jnp.concatenate([blank, even], axis=1)], axis=0
+    )
+
+
+def front_kernel(group_ref, sibling_ref, pair_ref, w_ref, averages_ref, normed_ref, out_ref):
+    normed_ref[0] = normalize(group_ref[0])
+    normed_ref[1] = normalize(sibling_ref[0])
     cols, keys, channels = pair_ref.shape
     heads = w_ref.shape[0]
     half = cols // 2
@@ -64,9 +65,6 @@
     w_sum = jnp.sum(w, axis=1, keepdims=True)
     even = jnp.full((channels, channels), 1.0 / channels, jnp.bfloat16)
     blank = jnp.zeros((channels, channels), jnp.bfloat16)
-    averages = jnp.concatenate(
-        [jnp.concatenate([even, blank], axis=1), jnp.concatenate([blank, even], axis=1)], axis=0
-    )
     pieces = jnp.concatenate([w_high, w_mid, rest.astype(jnp.bfloat16), even[:8]], axis=0)
     left = jnp.concatenate(
         [
@@ -81,7 +79,7 @@
     twins = jnp.concatenate(
         [jnp.concatenate(tiles[low : low + 2], axis=1) for low in range(0, half, 2)], axis=0
     )
-    means = dot(twins, averages)
+    means = dot(twins, averages_ref[...])
     products = lax.dot_general(twins, left, NT, preferred_element_type=jnp.float32)
     height = 2 * keys
     lane = lax.broadcasted_iota(jnp.int32, (height, 128), 1)
@@ -102,27 +100,26 @@
             out_ref[pl.ds((at // 8) * 8 * heads + at % 8, heads, stride=8), :] = bias[0:heads]
 
 
-def place_blocks(sources, origins, w_kv, key_ref, value_ref):
+def place_blocks(sources, origins, w_value, rows_ref, value_ref):
     _, rows, cols, channels = sources[0].shape
-    width = value_ref.shape[2]
     me = lax.axis_index("row")
-    for ref, entry, (flip, odd, even) in [
+    for ref, entry, (flip, odd, even, raw) in [
         (ref, entry, origin)
         for ref, group in zip(sources, origins)
         for entry, origin in enumerate(group)
     ]:
-        block = ref[entry].reshape(rows * cols, channels)
+        block = normalize(ref[entry]) if raw else ref[entry]
         core = me & 1
         chip = (me >> 1) ^ jnp.where(core == 1, odd, even)
         place = pl.ds(pl.multiple_of((2 * chip + (core ^ flip)) * cols, cols), cols)
-        kv = dot(block, w_kv).astype(jnp.bfloat16).reshape(rows, cols, 2 * width)
-        key_ref[:, place, :] = kv[:, :, :width]
-        value_ref[:, place, :] = kv[:, :, width:]
+        rows_ref[:, place, :] = block
+        value = dot(block.reshape(rows * cols, channels), w_value).astype(jnp.bfloat16)
+        value_ref[:, place, :] = value.reshape(rows, cols, value.shape[1])
 
 
 def early_kernel(heads, origins, *refs):
     sources = refs[: len(origins)]
-    wq_ref, wk_ref, wv_ref, wg_ref, key_ref, value_ref, gate_ref, stack_ref = refs[len(origins) :]
+    wq_ref, wk_ref, wv_ref, wg_ref, rows_ref, value_ref, gate_ref, stack_ref = refs[len(origins) :]
     _, rows, cols, channels = sources[0].shape
     width = wq_ref.shape[1]
     depth = width // heads
@@ -137,19 +134,20 @@
             tile = query[row * cols + g * 8 : row * cols + g * 8 + 8]
             for h in range(heads):
                 tiles.append(jnp.where(lane == h, tile, 0.0))
-        stack_ref[row] = jnp.concatenate(tiles, axis=0).astype(jnp.bfloat16)
-    w_kv = jnp.concatenate([wk_ref[...], wv_ref[...]], axis=1)
-    place_blocks(sources, origins, w_kv, key_ref, value_ref)
+        stacked = jnp.concatenate(tiles, axis=0).astype(jnp.bfloat16)
+        stack_ref[row] = lax.dot_general(
+            stacked, wk_ref[...], NT, preferred_element_type=jnp.float32
+        ).astype(jnp.bfloat16)
+    place_blocks(sources, origins, wv_ref[...], rows_ref, value_ref)
 
 
 def scores_kernel(origins, *refs):
     sources = refs[: len(origins)]
-    stack_ref, wk_ref, wv_ref, _, _, score_ref, key_ref, value_ref = refs[len(origins) :]
-    w_kv = jnp.concatenate([wk_ref[...], wv_ref[...]], axis=1)
-    place_blocks(sources, origins, w_kv, key_ref, value_ref)
+    stack_ref, wv_ref, _, _, score_ref, rows_ref, value_ref = refs[len(origins) :]
+    place_blocks(sources, origins, wv_ref[...], rows_ref, value_ref)
     for row in range(stack_ref.shape[0]):
         score_ref[row] = lax.dot_general(
-            stack_ref[row], key_ref[row], NT, preferred_element_type=jnp.float32
+            stack_ref[row], rows_ref[row], NT, preferred_element_type=jnp.float32
         )
 
 
@@ -230,45 +228,43 @@
 
 
 def col_plan(col_size):
-    return [1], pair_up(list(reversed(range(2, col_size))))
+    distances = list(reversed(range(1, col_size)))
+    middle = col_size // 2
+    distances.remove(middle)
+    return [middle], pair_up(distances)
 
 
 def per_device(row_size, col_size, pair, group, w_query, w_key, w_value, w_gate, w_bias, w_out):
     heads = w_bias.shape[1]
-    rows, cols, _ = group.shape
+    rows, cols, channels = group.shape
     width = w_query.shape[1]
     keys = pair.shape[1]
     all_keys = row_size * cols
     shape = jax.ShapeDtypeStruct
-    inputs = [pltpu.with_memory_space_constraint(a, pltpu.HBM) for a in (group, pair, w_bias.T)]
-    normed, pair, w_bias = call(
-        load_kernel,
+    averages = call(seed_kernel, shape((2 * channels, 2 * channels), jnp.bfloat16), [], HINT)
+    single, plan = row_plan(row_size)
+    raw = group[None]
+    sibling = swap(raw, row_size)
+    early, late = [], []
+    for s in single:
+        arrived = chip_shift(raw, row_size, s, s)
+        early.append((arrived, [(0, s, s, True)]))
+        late.append((swap(arrived, row_size), [(1, s, s, True)]))
+    both, panel = call(
+        front_kernel,
         (
-            shape(group.shape, jnp.bfloat16),
-            shape(pair.shape, pair.dtype),
-            shape(inputs[2].shape, jnp.float32),
+            shape((2,) + group.shape, jnp.bfloat16),
+            shape((cols * heads // 2, 2 * keys), jnp.float32),
         ),
-        inputs,
-        10**8,
-        [pltpu.VMEM(group.shape, group.dtype), pltpu.SemaphoreType.DMA((3,))],
-        pltpu.HBM,
-    )
-    panel = call(
-        bias_kernel, shape((cols * heads // 2, 2 * keys), jnp.float32), [pair, w_bias], 2 * 10**9
-    )
-    normed = normed[None]
-    sibling = swap(normed, row_size)
-    stacks, origins = [normed, sibling], [[(0, 0, 0)], [(1, 0, 0)]]
-    single, plan = row_plan(row_size)
-    for s in single:
-        arrived = chip_shift(normed, row_size, s, s)
-        stacks += [arrived, swap(arrived, row_size)]
-        origins += [[(0, s, s)], [(1, s, s)]]
-    both = jnp.concatenate([normed, sibling], axis=0)
+        [raw, sibling, pair, w_bias.T, averages],
+        2 * 10**9,
+    )
+    early.insert(0, (both, [(0, 0, 0, False), (1, 0, 0, False)]))
     for s, t in plan:
         arrived = chip_shift(both, row_size, s, t)
-        stacks += [arrived, swap(arrived, row_size)]
-        origins += [[(0, s, t), (1, s, t)], [(1, t, s), (0, t, s)]]
+        early.append((arrived, [(0, s, t, False), (1, s, t, False)]))
+        passed = swap(arrived, row_size)
+        late.append((passed, [(1, t, s, False), (0, t, s, False)]))
     near, distant = col_plan(col_size)
     panels = [panel]
     for s in near:
@@ -277,24 +273,23 @@
     for s, t in distant:
         arrived = col_shift(both, row_size, col_size, s, t)
         panels += [arrived, swap(arrived, row_size)]
-    keys_shape = shape((rows, all_keys, width), jnp.bfloat16)
-    soon = [0, 1] + list(range(2, len(stacks), 2))
-    late = list(range(3, len(stacks), 2))
-    key, value, gate, queries = call(
-        lambda *refs: early_kernel(heads, [origins[i] for i in soon], *refs),
+    keys_shape = shape((rows, all_keys, channels), jnp.bfloat16)
+    value_shape = shape((rows, all_keys, width), jnp.bfloat16)
+    normed, value, gate, queries = call(
+        lambda *refs: early_kernel(heads, [origin for _, origin in early], *refs),
         (
             keys_shape,
-            keys_shape,
+            value_shape,
             shape((rows, cols, width), jnp.float32),
-            shape((rows, cols * heads, width), jnp.bfloat16),
+            shape((rows, cols * heads, channels), jnp.bfloat16),
         ),
-        [stacks[i] for i in soon] + [w_query, w_key, w_value, w_gate],
+        [block for block, _ in early] + [w_query, w_key, w_value, w_gate],
         10**9,
     )
-    late_args = [stacks[i] for i in late] + [queries, w_key, w_value, key, value]
+    late_args = [block for block, _ in late] + [queries, w_value, normed, value]
     scores, _, value = call(
-        lambda *refs: scores_kernel([origins[i] for i in late], *refs),
-        (shape((rows, cols * heads, all_keys), jnp.float32), keys_shape, keys_shape),
+        lambda *refs: scores_kernel([origin for _, origin in late], *refs),
+        (shape((rows, cols * heads, all_keys), jnp.float32), keys_shape, value_shape),
         late_args,
         10**9,
         aliases={len(late_args) - 2: 1, len(late_args) - 1: 2},

time: 16.6 us -> 17.7 us (1.066)
  waiting for transfers between devices: 2.93 us -> 4.56 us
  Pallas kernels: 4.08 us -> 3.02 us
  starting transfers between devices: 9.25 us -> 9.88 us
    ppermute x2, waiting for transfers between devices: 1.46 us -> 2.81 us  [chip_shift(): return lax.ppermute(value, 'row', pairs)]
    pallas_call x5, Pallas kernels: 4.08 us -> 3.02 us  [call(): pl.pallas_call(kernel, out_shape=outs, in_specs=[pl.BlockSpec(memory_spac...]
    ppermute x5, waiting for transfers between devices: 0.42 us -> 1.32 us  [swap(): return lax.ppermute(value, 'row', [(i, i ^ 1) for i in range(size)])]
    ppermute x2, waiting for transfers between devices: 1.05 us -> 0.43 us  [col_shift(): return lax.ppermute(value, ('row', 'col'), pairs)]
    ppermute x5, starting transfers between devices: 1.01 us -> 1.5 us  [swap(): return lax.ppermute(value, 'row', [(i, i ^ 1) for i in range(size)])]
  transfers between devices with their start and end apart: 9 -> 9, of which waited for: 4 -> 4; matrix products, arithmetic and copies ran while one was open for 0% -> 0% of each run, Pallas kernels for 11% -> 6%
where the time goes in v3:
time: 17.7 us; the launch traced here: 17.5 us
  starting transfers between devices  9.88 us (56%)
  waiting for transfers between devices  4.56 us (26%)
  Pallas kernels  3.02 us (17%)
    ppermute x2, starting transfers between devices, col_shift(): return lax.ppermute(value, ('row', 'col'), pairs)  4.23 us
    ppermute x2, starting transfers between devices, chip_shift(): return lax.ppermute(value, 'row', pairs)  4.15 us
    pallas_call x5, Pallas kernels, call(): pl.pallas_call(kernel, out_shape=outs, in_specs=[pl.BlockSpec(memory_spac...  3.02 us
    ppermute x2, waiting for transfers between devices, chip_shift(): return lax.ppermute(value, 'row', pairs)  2.81 us
    ppermute x5, starting transfers between devices, swap(): return lax.ppermute(value, 'row', [(i, i ^ 1) for i in range(size)])  1.5 us
    ppermute x5, waiting for transfers between devices, swap(): return lax.ppermute(value, 'row', [(i, i ^ 1) for i in range(size)])  1.32 us
    ppermute x2, waiting for transfers between devices, col_shift(): return lax.ppermute(value, ('row', 'col'), pairs)  0.43 us
  transfers between devices with their start and end apart: 9, of which 4 were waited for; matrix products, arithmetic and copies ran while one was open for 0% of the time, Pallas kernels for 6%

profile of v3, /device:TPU:0, one launch (start us, length us, event | category | flops | bytes accessed | tf_op | source)
XLA Modules:
  0.0 17.5 jit_solution(4413618857743802342)
XLA Ops:
  0.0 0.0 copy-start
  0.0 0.0 copy-start.1
  0.0 0.0 copy-start.7
  0.0 0.6 %collective-permute-start = (bf16[1,8,32,128]{3,2,1,0:T(8,128)(2,1)}, bf16[1,8,32,128]{3,2,1,0:T(8,128)(2,1)S(1)}, u32[]{:S(2)}, u32[]{:S(2)}) collective-permute-start(bf16[1,8,32,128]{3,2,1,0:T(8,128)(2,1)} %bitcast.2), channel_id=1, source_target_pairs={{0,4},{4,0},{8,12},{12,8},{16,20},{20,16},{24,28},{28,24},{1,5},{5... | collective-permute-start | bytes 196616 | tf_op jit(solution)/shard_map/ppermute | solution.py:204
  0.6 1.1 %collective-permute-done.sibling_ref = bf16[1,8,32,128]{3,2,1,0:T(8,128)(2,1)S(1)} collective-permute-done((bf16[1,8,32,128]{3,2,1,0:T(8,128)(2,1)}, bf16[1,8,32,128]{3,2,1,0:T(8,128)(2,1)S(1)}, u32[]{:S(2)}, u32[]{:S(2)}) %collective-permute-start) | collective-permute-done | bytes 65568 | tf_op jit(solution)/shard_map/ppermute | solution.py:204
  1.7 0.0 copy-done
  1.7 0.0 copy-done.1
  1.7 0.0 copy-done.7
  1.7 0.8 %shard_map.83 = (bf16[2,8,32,128]{3,2,1,0:T(8,128)(2,1)S(1)}, f32[64,128]{1,0:T(8,128)S(1)}) custom-call(bf16[1,8,32,128]{3,2,1,0:T(8,128)(2,1)S(1)} %bitcast.3, bf16[1,8,32,128]{3,2,1,0:T(8,128)(2,1)S(1)} %collective-permute-done.sibling_ref, bf16[32,64,128]{2,1,0:T(8,128)(2,1)S(1)} %copy-done, f32[4,128]{1,0:T(4,128)S(1)} %bitcast.5, ...), custom_call_target="tpu_custom_call" | custom-call | flops 2000000000 | bytes 1048576 | tf_op jit(solution)/shard_map/pallas_call | solution.py:19
  2.5 0.4 %collective-permute-start.2 = (f32[64,128]{1,0:T(8,128)S(1)}, f32[64,128]{1,0:T(8,128)S(1)}, u32[]{:S(2)}, u32[]{:S(2)}) collective-permute-start(f32[64,128]{1,0:T(8,128)S(1)} %get-tuple-element.13.refs_0_), channel_id=1, source_target_pairs={{0,4},{4,0},{8,12},{12,8},{16,20},{20,16},{24,28},{28,24},{1,5},{5... | collective-permute-start | bytes 98312 | tf_op jit(solution)/shard_map/ppermute | solution.py:204
  2.9 3.6 %collective-permute-start.5 = (bf16[1,8,32,128]{3,2,1,0:T(8,128)(2,1)S(1)}, bf16[1,8,32,128]{3,2,1,0:T(8,128)(2,1)S(1)}, u32[]{:S(2)}, u32[]{:S(2)}) collective-permute-start(bf16[1,8,32,128]{3,2,1,0:T(8,128)(2,1)S(1)} %bitcast.4), channel_id=1, source_target_pairs={{0,24},{4,28},{8,16},{12,20},{16,8},{20,12},{24,0},{28,4},{1,25},{... | collective-permute-start | bytes 196616 | tf_op jit(solution)/shard_map/ppermute | solution.py:209
  6.5 0.0 copy-start.2
  6.5 0.0 copy-start.3
  6.5 0.0 copy-start.4
  6.5 0.0 copy-start.5
  6.5 0.6 %collective-permute-start.7 = (bf16[2,8,32,128]{3,2,1,0:T(8,128)(2,1)S(1)}, bf16[2,8,32,128]{3,2,1,0:T(8,128)(2,1)S(1)}, u32[]{:S(2)}, u32[]{:S(2)}) collective-permute-start(bf16[2,8,32,128]{3,2,1,0:T(8,128)(2,1)S(1)} %get-tuple-element.14.refs_0_), channel_id=1, source_target_pairs={{0,16},{4,12},{8,24},{12,4},{16,0},{20,28},{24,8},{28,20},{1,17},{... | collective-permute-start | bytes 393224 | tf_op jit(solution)/shard_map/ppermute | solution.py:209
  7.1 0.0 collective-permute-done.2
  7.1 1.6 %collective-permute-start.3 = (f32[128,128]{1,0:T(8,128)S(1)}, f32[128,128]{1,0:T(8,128)S(1)}, u32[]{:S(2)}, u32[]{:S(2)}) collective-permute-start(f32[128,128]{1,0:T(8,128)S(1)} %pad_maximum_fusion), channel_id=1, source_target_pairs={{0,1},{1,0},{2,3},{3,2},{4,7},{5,6},{6,5},{7,4},{8,9},{9,8},{10,11... | collective-permute-start | bytes 196616 | tf_op jit(solution)/shard_map/ppermute | solution.py:218
  8.7 2.8 %collective-permute-done.7.refs_2_ = bf16[2,8,32,128]{3,2,1,0:T(8,128)(2,1)S(1)} collective-permute-done((bf16[2,8,32,128]{3,2,1,0:T(8,128)(2,1)S(1)}, bf16[2,8,32,128]{3,2,1,0:T(8,128)(2,1)S(1)}, u32[]{:S(2)}, u32[]{:S(2)}) %collective-permute-start.7) | collective-permute-done | bytes 131104 | tf_op jit(solution)/shard_map/ppermute | solution.py:209
  11.5 0.0 collective-permute-start.8
  11.5 2.6 %collective-permute-start.1 = (f32[64,128]{1,0:T(8,128)S(1)}, f32[64,128]{1,0:T(8,128)S(1)}, u32[]{:S(2)}, u32[]{:S(2)}) collective-permute-start(f32[64,128]{1,0:T(8,128)S(1)} %get-tuple-element.13.refs_0_), channel_id=1, source_target_pairs={{0,2},{1,3},{2,0},{3,1},{4,6},{5,7},{6,4},{7,5},{8,10},{9,11},{10,... | collective-permute-start | bytes 98312 | tf_op jit(solution)/shard_map/ppermute | solution.py:218
  14.1 0.0 collective-permute-done.5.refs_1_
  14.1 0.2 %collective-permute-start.6 = (bf16[1,8,32,128]{3,2,1,0:T(8,128)(2,1)S(1)}, bf16[1,8,32,128]{3,2,1,0:T(8,128)(2,1)S(1)}, u32[]{:S(2)}, u32[]{:S(2)}) collective-permute-start(bf16[1,8,32,128]{3,2,1,0:T(8,128)(2,1)S(1)} %collective-permute-done.5.refs_1_), channel_id=1, source_target_pairs={{0,4},{4,0},{8,12},{12,8},{16,20},{20,16},{24,28},{28,24},{1,5},{5... | collective-permute-start | bytes 196616 | tf_op jit(solution)/shard_map/ppermute | solution.py:204
  14.3 0.0 collective-permute-done.3.refs_2_
  14.3 0.3 %collective-permute-start.4 = (f32[128,128]{1,0:T(8,128)S(1)}, f32[128,128]{1,0:T(8,128)S(1)}, u32[]{:S(2)}, u32[]{:S(2)}) collective-permute-start(f32[128,128]{1,0:T(8,128)S(1)} %collective-permute-done.3.refs_2_), channel_id=1, source_target_pairs={{0,4},{4,0},{8,12},{12,8},{16,20},{20,16},{24,28},{28,24},{1,5},{5... | collective-permute-start | bytes 196616 | tf_op jit(solution)/shard_map/ppermute | solution.py:204
  14.6 0.0 copy-done.2
  14.6 0.0 copy-done.3
  14.6 0.0 copy-done.4
  14.6 0.0 copy-done.5
  14.6 0.5 %shard_map.84 = (bf16[8,256,128]{2,1,0:T(8,128)(2,1)S(1)}, bf16[8,256,128]{2,1,0:T(8,128)(2,1)S(1)}, f32[8,32,128]{2,1,0:T(8,128)S(1)}, bf16[8,128,128]{2,1,0:T(8,128)(2,1)S(1)}) custom-call(bf16[2,8,32,128]{3,2,1,0:T(8,128)(2,1)S(1)} %get-tuple-element.14.refs_0_, bf16[1,8,32,128]{3,2,1,0:T(8,128)(2,1)S(1)} %collective-permute-done.5.refs_1_, ...), custom_call_target="tpu_custom_call" | custom-call | flops 1000000000 | bytes 1048576 | tf_op jit(solution)/shard_map/pallas_call | solution.py:19
  15.2 0.2 %collective-permute-done.6.refs_0_ = bf16[1,8,32,128]{3,2,1,0:T(8,128)(2,1)S(1)} collective-permute-done((bf16[1,8,32,128]{3,2,1,0:T(8,128)(2,1)S(1)}, bf16[1,8,32,128]{3,2,1,0:T(8,128)(2,1)S(1)}, u32[]{:S(2)}, u32[]{:S(2)}) %collective-permute-start.6) | collective-permute-done | bytes 65568 | tf_op jit(solution)/shard_map/ppermute | solution.py:204
  15.4 0.0 collective-permute-done.8.refs_1_
  15.4 0.0 copy-start.6
  15.4 0.5 %shard_map.85 = (f32[8,128,256]{2,1,0:T(8,128)S(1)}, bf16[8,256,128]{2,1,0:T(8,128)(2,1)S(1)}, bf16[8,256,128]{2,1,0:T(8,128)(2,1)S(1)}) custom-call(bf16[1,8,32,128]{3,2,1,0:T(8,128)(2,1)S(1)} %collective-permute-done.6.refs_0_, bf16[2,8,32,128]{3,2,1,0:T(8,128)(2,1)S(1)} %collective-permute-done.8.refs_1_, ...), custom_call_target="tpu_custom_call", output_to_operand_aliasing={{1}: (4, {}), {2}: (5, {})} | custom-call | flops 1000000000 | bytes 1048576 | tf_op jit(solution)/shard_map/pallas_call | solution.py:19
  15.9 0.4 %collective-permute-done.1.refs_1_ = f32[64,128]{1,0:T(8,128)S(1)} collective-permute-done((f32[64,128]{1,0:T(8,128)S(1)}, f32[64,128]{1,0:T(8,128)S(1)}, u32[]{:S(2)}, u32[]{:S(2)}) %collective-permute-start.1) | collective-permute-done | bytes 32800 | tf_op jit(solution)/shard_map/ppermute | solution.py:218
  16.3 0.0 collective-permute-done.4.refs_3_
  16.3 0.0 copy-done.6
  16.3 1.2 %shard_map.86 = bf16[8,32,128]{2,1,0:T(8,128)(2,1)} custom-call(f32[64,128]{1,0:T(8,128)S(1)} %get-tuple-element.13.refs_0_, f32[64,128]{1,0:T(8,128)S(1)} %collective-permute-done.1.refs_1_, f32[128,128]{1,0:T(8,128)S(1)} %collective-permute-done.3.refs_2_, f32[128,128]{1,0:T(8,128)S(1)} %collective-permute-done.4.refs_3_, ...), custom_call_target="tpu_custom_call" | custom-call | flops 1000000000 | bytes 1048576 | tf_op jit(solution)/shard_map/pallas_call | solution.py:19
  (2 shorter events, 0.0 us)
Async XLA Ops:
  0.0 1.7 %copy-start = (bf16[32,64,128]{2,1,0:T(8,128)(2,1)S(1)}, bf16[32,64,128]{2,1,0:T(8,128)(2,1)}, u32[]{:S(2)}) copy-start(bf16[32,64,128]{2,1,0:T(8,128)(2,1)} %pair_ref.1) | copy-start | bytes 1572868
  0.0 1.7 %copy-start.1 = (bf16[8,32,128]{2,1,0:T(8,128)(2,1)S(1)}, bf16[8,32,128]{2,1,0:T(8,128)(2,1)}, u32[]{:S(2)}) copy-start(bf16[8,32,128]{2,1,0:T(8,128)(2,1)} %param.9) | copy-start | bytes 196612
  0.0 1.7 %copy-start.7 = (f32[128,4]{0,1:T(4,128)S(1)}, f32[128,4]{0,1:T(4,128)}, u32[]{:S(2)}) copy-start(f32[128,4]{0,1:T(4,128)} %param.14) | copy-start | bytes 6148
  0.0 1.7 %collective-permute-start = (bf16[1,8,32,128]{3,2,1,0:T(8,128)(2,1)}, bf16[1,8,32,128]{3,2,1,0:T(8,128)(2,1)S(1)}, u32[]{:S(2)}, u32[]{:S(2)}) collective-permute-start(bf16[1,8,32,128]{3,2,1,0:T(8,128)(2,1)} %bitcast.2), channel_id=1, source_target_pairs={{0,4},{4,0},{8,12},{12,8},{16,20},{20,16},{24,28},{28,24},{1,5},{5... | collective-permute-start | bytes 196616 | tf_op jit(solution)/shard_map/ppermute | solution.py:204
  2.5 4.6 %collective-permute-start.2 = (f32[64,128]{1,0:T(8,128)S(1)}, f32[64,128]{1,0:T(8,128)S(1)}, u32[]{:S(2)}, u32[]{:S(2)}) collective-permute-start(f32[64,128]{1,0:T(8,128)S(1)} %get-tuple-element.13.refs_0_), channel_id=1, source_target_pairs={{0,4},{4,0},{8,12},{12,8},{16,20},{20,16},{24,28},{28,24},{1,5},{5... | collective-permute-start | bytes 98312 | tf_op jit(solution)/shard_map/ppermute | solution.py:204
  2.9 11.2 %collective-permute-start.5 = (bf16[1,8,32,128]{3,2,1,0:T(8,128)(2,1)S(1)}, bf16[1,8,32,128]{3,2,1,0:T(8,128)(2,1)S(1)}, u32[]{:S(2)}, u32[]{:S(2)}) collective-permute-start(bf16[1,8,32,128]{3,2,1,0:T(8,128)(2,1)S(1)} %bitcast.4), channel_id=1, source_target_pairs={{0,24},{4,28},{8,16},{12,20},{16,8},{20,12},{24,0},{28,4},{1,25},{... | collective-permute-start | bytes 196616 | tf_op jit(solution)/shard_map/ppermute | solution.py:209
  6.5 8.2 %copy-start.2 = (bf16[128,128]{1,0:T(8,128)(2,1)S(1)}, bf16[128,128]{1,0:T(8,128)(2,1)}, u32[]{:S(2)}) copy-start(bf16[128,128]{1,0:T(8,128)(2,1)} %refs_3_.2) | copy-start | bytes 98308
  6.5 8.2 %copy-start.3 = (bf16[128,128]{1,0:T(8,128)(2,1)S(1)}, bf16[128,128]{1,0:T(8,128)(2,1)}, u32[]{:S(2)}) copy-start(bf16[128,128]{1,0:T(8,128)(2,1)} %refs_4_.1) | copy-start | bytes 98308
  6.5 8.2 %copy-start.4 = (bf16[128,128]{1,0:T(8,128)(2,1)S(1)}, bf16[128,128]{1,0:T(8,128)(2,1)}, u32[]{:S(2)}) copy-start(bf16[128,128]{1,0:T(8,128)(2,1)} %refs_6_.1) | copy-start | bytes 98308
  6.5 8.2 %copy-start.5 = (bf16[128,128]{1,0:T(8,128)(2,1)S(1)}, bf16[128,128]{1,0:T(8,128)(2,1)}, u32[]{:S(2)}) copy-start(bf16[128,128]{1,0:T(8,128)(2,1)} %refs_3_.3) | copy-start | bytes 98308
  6.5 5.0 %collective-permute-start.7 = (bf16[2,8,32,128]{3,2,1,0:T(8,128)(2,1)S(1)}, bf16[2,8,32,128]{3,2,1,0:T(8,128)(2,1)S(1)}, u32[]{:S(2)}, u32[]{:S(2)}) collective-permute-start(bf16[2,8,32,128]{3,2,1,0:T(8,128)(2,1)S(1)} %get-tuple-element.14.refs_0_), channel_id=1, source_target_pairs={{0,16},{4,12},{8,24},{12,4},{16,0},{20,28},{24,8},{28,20},{1,17},{... | collective-permute-start | bytes 393224 | tf_op jit(solution)/shard_map/ppermute | solution.py:209
  7.1 7.3 %collective-permute-start.3 = (f32[128,128]{1,0:T(8,128)S(1)}, f32[128,128]{1,0:T(8,128)S(1)}, u32[]{:S(2)}, u32[]{:S(2)}) collective-permute-start(f32[128,128]{1,0:T(8,128)S(1)} %pad_maximum_fusion), channel_id=1, source_target_pairs={{0,1},{1,0},{2,3},{3,2},{4,7},{5,6},{6,5},{7,4},{8,9},{9,8},{10,11... | collective-permute-start | bytes 196616 | tf_op jit(solution)/shard_map/ppermute | solution.py:218
  11.5 3.9 %collective-permute-start.8 = (bf16[2,8,32,128]{3,2,1,0:T(8,128)(2,1)S(1)}, bf16[2,8,32,128]{3,2,1,0:T(8,128)(2,1)S(1)}, u32[]{:S(2)}, u32[]{:S(2)}) collective-permute-start(bf16[2,8,32,128]{3,2,1,0:T(8,128)(2,1)S(1)} %collective-permute-done.7.refs_2_), channel_id=1, source_target_pairs={{0,4},{4,0},{8,12},{12,8},{16,20},{20,16},{24,28},{28,24},{1,5},{5... | collective-permute-start | bytes 393224 | tf_op jit(solution)/shard_map/ppermute | solution.py:204
  11.5 4.8 %collective-permute-start.1 = (f32[64,128]{1,0:T(8,128)S(1)}, f32[64,128]{1,0:T(8,128)S(1)}, u32[]{:S(2)}, u32[]{:S(2)}) collective-permute-start(f32[64,128]{1,0:T(8,128)S(1)} %get-tuple-element.13.refs_0_), channel_id=1, source_target_pairs={{0,2},{1,3},{2,0},{3,1},{4,6},{5,7},{6,4},{7,5},{8,10},{9,11},{10,... | collective-permute-start | bytes 98312 | tf_op jit(solution)/shard_map/ppermute | solution.py:218
  14.1 1.3 %collective-permute-start.6 = (bf16[1,8,32,128]{3,2,1,0:T(8,128)(2,1)S(1)}, bf16[1,8,32,128]{3,2,1,0:T(8,128)(2,1)S(1)}, u32[]{:S(2)}, u32[]{:S(2)}) collective-permute-start(bf16[1,8,32,128]{3,2,1,0:T(8,128)(2,1)S(1)} %collective-permute-done.5.refs_1_), channel_id=1, source_target_pairs={{0,4},{4,0},{8,12},{12,8},{16,20},{20,16},{24,28},{28,24},{1,5},{5... | collective-permute-start | bytes 196616 | tf_op jit(solution)/shard_map/ppermute | solution.py:204
  14.3 2.0 %collective-permute-start.4 = (f32[128,128]{1,0:T(8,128)S(1)}, f32[128,128]{1,0:T(8,128)S(1)}, u32[]{:S(2)}, u32[]{:S(2)}) collective-permute-start(f32[128,128]{1,0:T(8,128)S(1)} %collective-permute-done.3.refs_2_), channel_id=1, source_target_pairs={{0,4},{4,0},{8,12},{12,8},{16,20},{20,16},{24,28},{28,24},{1,5},{5... | collective-permute-start | bytes 196616 | tf_op jit(solution)/shard_map/ppermute | solution.py:204
  15.4 1.0 %copy-start.6 = (bf16[128,128]{1,0:T(8,128)(2,1)S(1)}, bf16[128,128]{1,0:T(8,128)(2,1)}, u32[]{:S(2)}) copy-start(bf16[128,128]{1,0:T(8,128)(2,1)} %refs_7_.1) | copy-start | bytes 98308

commit v4 on v3

--- a/solution.py
+++ b/solution.py
@@ -12,6 +12,7 @@
 NT = (((1,), (1,)), ((), ()))
 GRANT = 16 << 20
 HINT = 10**10
+LOG2E = math.log2(math.e)
 VMEM = pl.BlockSpec(memory_space=pltpu.VMEM)
 
 
@@ -95,7 +96,7 @@
         for twin in range(2):
             t = mixed[twin * 64 : twin * 64 + 64]
             total = t[0:8] + t[8:16] + t[16:24] - t[24:32] * w_sum
-            bias = total * lax.rsqrt(t[32:40] * (1.0 / channels) + EPS)
+            bias = total * (lax.rsqrt(t[32:40] * (1.0 / channels) + EPS) * LOG2E)
             at = low + twin
             out_ref[pl.ds((at // 8) * 8 * heads + at % 8, heads, stride=8), :] = bias[0:heads]
 
@@ -135,9 +136,10 @@
             for h in range(heads):
                 tiles.append(jnp.where(lane == h, tile, 0.0))
         stacked = jnp.concatenate(tiles, axis=0).astype(jnp.bfloat16)
-        stack_ref[row] = lax.dot_general(
+        turned = lax.dot_general(
             stacked, wk_ref[...], NT, preferred_element_type=jnp.float32
-        ).astype(jnp.bfloat16)
+        )
+        stack_ref[row] = (turned * LOG2E).astype(jnp.bfloat16)
     place_blocks(sources, origins, wv_ref[...], rows_ref, value_ref)
 
 
@@ -183,7 +185,7 @@
     for row in range(rows):
         scores = score_ref[row] + bias_ref[...]
         top = jnp.max(scores, axis=1, keepdims=True)
-        weights = jnp.exp(scores - top).astype(jnp.bfloat16)
+        weights = jnp.exp2(scores - top).astype(jnp.bfloat16)
         both = dot(weights, jnp.concatenate([value_ref[row], ones], axis=1))
         for g in range(cols // 8):
             base = g * heads * 8

time: 17.7 us -> 17.7 us (level)
  no operation moved by 1% of the time
where the time goes in v4:
time: 17.7 us; the launch traced here: 17.6 us
  starting transfers between devices  9.88 us (56%)
  waiting for transfers between devices  4.56 us (26%)
  Pallas kernels  3.03 us (17%)
    ppermute x2, starting transfers between devices, col_shift(): return lax.ppermute(value, ('row', 'col'), pairs)  4.23 us
    ppermute x2, starting transfers between devices, chip_shift(): return lax.ppermute(value, 'row', pairs)  4.15 us
    pallas_call x5, Pallas kernels, call(): pl.pallas_call(kernel, out_shape=outs, in_specs=[pl.BlockSpec(memory_spac...  3.03 us
    ppermute x2, waiting for transfers between devices, chip_shift(): return lax.ppermute(value, 'row', pairs)  2.81 us
    ppermute x5, starting transfers between devices, swap(): return lax.ppermute(value, 'row', [(i, i ^ 1) for i in range(size)])  1.5 us
    ppermute x5, waiting for transfers between devices, swap(): return lax.ppermute(value, 'row', [(i, i ^ 1) for i in range(size)])  1.32 us
    ppermute x2, waiting for transfers between devices, col_shift(): return lax.ppermute(value, ('row', 'col'), pairs)  0.43 us
  transfers between devices with their start and end apart: 9, of which 4 were waited for; matrix products, arithmetic and copies ran while one was open for 0% of the time, Pallas kernels for 6%

profile of v4, /device:TPU:0, one launch (start us, length us, event | category | flops | bytes accessed | tf_op | source)
XLA Modules:
  0.0 17.6 jit_solution(15659158714280092637)
XLA Ops:
  0.0 0.0 copy-start
  0.0 0.0 copy-start.1
  0.0 0.0 copy-start.7
  0.0 0.6 %collective-permute-start = (bf16[1,8,32,128]{3,2,1,0:T(8,128)(2,1)}, bf16[1,8,32,128]{3,2,1,0:T(8,128)(2,1)S(1)}, u32[]{:S(2)}, u32[]{:S(2)}) collective-permute-start(bf16[1,8,32,128]{3,2,1,0:T(8,128)(2,1)} %bitcast.2), channel_id=1, source_target_pairs={{0,4},{4,0},{8,12},{12,8},{16,20},{20,16},{24,28},{28,24},{1,5},{5... | collective-permute-start | bytes 196616 | tf_op jit(solution)/shard_map/ppermute | solution.py:206
  0.6 1.1 %collective-permute-done.sibling_ref = bf16[1,8,32,128]{3,2,1,0:T(8,128)(2,1)S(1)} collective-permute-done((bf16[1,8,32,128]{3,2,1,0:T(8,128)(2,1)}, bf16[1,8,32,128]{3,2,1,0:T(8,128)(2,1)S(1)}, u32[]{:S(2)}, u32[]{:S(2)}) %collective-permute-start) | collective-permute-done | bytes 65568 | tf_op jit(solution)/shard_map/ppermute | solution.py:206
  1.7 0.0 copy-done
  1.7 0.0 copy-done.1
  1.7 0.0 copy-done.7
  1.7 0.8 %shard_map.83 = (bf16[2,8,32,128]{3,2,1,0:T(8,128)(2,1)S(1)}, f32[64,128]{1,0:T(8,128)S(1)}) custom-call(bf16[1,8,32,128]{3,2,1,0:T(8,128)(2,1)S(1)} %bitcast.3, bf16[1,8,32,128]{3,2,1,0:T(8,128)(2,1)S(1)} %collective-permute-done.sibling_ref, bf16[32,64,128]{2,1,0:T(8,128)(2,1)S(1)} %copy-done, f32[4,128]{1,0:T(4,128)S(1)} %bitcast.5, ...), custom_call_target="tpu_custom_call" | custom-call | flops 2000000000 | bytes 1048576 | tf_op jit(solution)/shard_map/pallas_call | solution.py:20
  2.5 0.4 %collective-permute-start.2 = (f32[64,128]{1,0:T(8,128)S(1)}, f32[64,128]{1,0:T(8,128)S(1)}, u32[]{:S(2)}, u32[]{:S(2)}) collective-permute-start(f32[64,128]{1,0:T(8,128)S(1)} %get-tuple-element.13.refs_0_), channel_id=1, source_target_pairs={{0,4},{4,0},{8,12},{12,8},{16,20},{20,16},{24,28},{28,24},{1,5},{5... | collective-permute-start | bytes 98312 | tf_op jit(solution)/shard_map/ppermute | solution.py:206
  2.9 3.6 %collective-permute-start.5 = (bf16[1,8,32,128]{3,2,1,0:T(8,128)(2,1)S(1)}, bf16[1,8,32,128]{3,2,1,0:T(8,128)(2,1)S(1)}, u32[]{:S(2)}, u32[]{:S(2)}) collective-permute-start(bf16[1,8,32,128]{3,2,1,0:T(8,128)(2,1)S(1)} %bitcast.4), channel_id=1, source_target_pairs={{0,24},{4,28},{8,16},{12,20},{16,8},{20,12},{24,0},{28,4},{1,25},{... | collective-permute-start | bytes 196616 | tf_op jit(solution)/shard_map/ppermute | solution.py:211
  6.5 0.0 copy-start.2
  6.5 0.0 copy-start.3
  6.5 0.0 copy-start.4
  6.5 0.0 copy-start.5
  6.5 0.6 %collective-permute-start.7 = (bf16[2,8,32,128]{3,2,1,0:T(8,128)(2,1)S(1)}, bf16[2,8,32,128]{3,2,1,0:T(8,128)(2,1)S(1)}, u32[]{:S(2)}, u32[]{:S(2)}) collective-permute-start(bf16[2,8,32,128]{3,2,1,0:T(8,128)(2,1)S(1)} %get-tuple-element.14.refs_0_), channel_id=1, source_target_pairs={{0,16},{4,12},{8,24},{12,4},{16,0},{20,28},{24,8},{28,20},{1,17},{... | collective-permute-start | bytes 393224 | tf_op jit(solution)/shard_map/ppermute | solution.py:211
  7.1 0.0 collective-permute-done.2
  7.1 1.6 %collective-permute-start.3 = (f32[128,128]{1,0:T(8,128)S(1)}, f32[128,128]{1,0:T(8,128)S(1)}, u32[]{:S(2)}, u32[]{:S(2)}) collective-permute-start(f32[128,128]{1,0:T(8,128)S(1)} %pad_maximum_fusion), channel_id=1, source_target_pairs={{0,1},{1,0},{2,3},{3,2},{4,7},{5,6},{6,5},{7,4},{8,9},{9,8},{10,11... | collective-permute-start | bytes 196616 | tf_op jit(solution)/shard_map/ppermute | solution.py:220
  8.7 2.8 %collective-permute-done.7.refs_2_ = bf16[2,8,32,128]{3,2,1,0:T(8,128)(2,1)S(1)} collective-permute-done((bf16[2,8,32,128]{3,2,1,0:T(8,128)(2,1)S(1)}, bf16[2,8,32,128]{3,2,1,0:T(8,128)(2,1)S(1)}, u32[]{:S(2)}, u32[]{:S(2)}) %collective-permute-start.7) | collective-permute-done | bytes 131104 | tf_op jit(solution)/shard_map/ppermute | solution.py:211
  11.5 0.0 collective-permute-start.8
  11.5 2.6 %collective-permute-start.1 = (f32[64,128]{1,0:T(8,128)S(1)}, f32[64,128]{1,0:T(8,128)S(1)}, u32[]{:S(2)}, u32[]{:S(2)}) collective-permute-start(f32[64,128]{1,0:T(8,128)S(1)} %get-tuple-element.13.refs_0_), channel_id=1, source_target_pairs={{0,2},{1,3},{2,0},{3,1},{4,6},{5,7},{6,4},{7,5},{8,10},{9,11},{10,... | collective-permute-start | bytes 98312 | tf_op jit(solution)/shard_map/ppermute | solution.py:220
  14.1 0.0 collective-permute-done.5.refs_1_
  14.1 0.2 %collective-permute-start.6 = (bf16[1,8,32,128]{3,2,1,0:T(8,128)(2,1)S(1)}, bf16[1,8,32,128]{3,2,1,0:T(8,128)(2,1)S(1)}, u32[]{:S(2)}, u32[]{:S(2)}) collective-permute-start(bf16[1,8,32,128]{3,2,1,0:T(8,128)(2,1)S(1)} %collective-permute-done.5.refs_1_), channel_id=1, source_target_pairs={{0,4},{4,0},{8,12},{12,8},{16,20},{20,16},{24,28},{28,24},{1,5},{5... | collective-permute-start | bytes 196616 | tf_op jit(solution)/shard_map/ppermute | solution.py:206
  14.3 0.0 collective-permute-done.3.refs_2_
  14.3 0.3 %collective-permute-start.4 = (f32[128,128]{1,0:T(8,128)S(1)}, f32[128,128]{1,0:T(8,128)S(1)}, u32[]{:S(2)}, u32[]{:S(2)}) collective-permute-start(f32[128,128]{1,0:T(8,128)S(1)} %collective-permute-done.3.refs_2_), channel_id=1, source_target_pairs={{0,4},{4,0},{8,12},{12,8},{16,20},{20,16},{24,28},{28,24},{1,5},{5... | collective-permute-start | bytes 196616 | tf_op jit(solution)/shard_map/ppermute | solution.py:206
  14.6 0.0 copy-done.2
  14.6 0.0 copy-done.3
  14.6 0.0 copy-done.4
  14.6 0.0 copy-done.5
  14.6 0.5 %shard_map.84 = (bf16[8,256,128]{2,1,0:T(8,128)(2,1)S(1)}, bf16[8,256,128]{2,1,0:T(8,128)(2,1)S(1)}, f32[8,32,128]{2,1,0:T(8,128)S(1)}, bf16[8,128,128]{2,1,0:T(8,128)(2,1)S(1)}) custom-call(bf16[2,8,32,128]{3,2,1,0:T(8,128)(2,1)S(1)} %get-tuple-element.14.refs_0_, bf16[1,8,32,128]{3,2,1,0:T(8,128)(2,1)S(1)} %collective-permute-done.5.refs_1_, ...), custom_call_target="tpu_custom_call" | custom-call | flops 1000000000 | bytes 1048576 | tf_op jit(solution)/shard_map/pallas_call | solution.py:20
  15.2 0.2 %collective-permute-done.6.refs_0_ = bf16[1,8,32,128]{3,2,1,0:T(8,128)(2,1)S(1)} collective-permute-done((bf16[1,8,32,128]{3,2,1,0:T(8,128)(2,1)S(1)}, bf16[1,8,32,128]{3,2,1,0:T(8,128)(2,1)S(1)}, u32[]{:S(2)}, u32[]{:S(2)}) %collective-permute-start.6) | collective-permute-done | bytes 65568 | tf_op jit(solution)/shard_map/ppermute | solution.py:206
  15.4 0.0 collective-permute-done.8.refs_1_
  15.4 0.0 copy-start.6
  15.4 0.5 %shard_map.85 = (f32[8,128,256]{2,1,0:T(8,128)S(1)}, bf16[8,256,128]{2,1,0:T(8,128)(2,1)S(1)}, bf16[8,256,128]{2,1,0:T(8,128)(2,1)S(1)}) custom-call(bf16[1,8,32,128]{3,2,1,0:T(8,128)(2,1)S(1)} %collective-permute-done.6.refs_0_, bf16[2,8,32,128]{3,2,1,0:T(8,128)(2,1)S(1)} %collective-permute-done.8.refs_1_, ...), custom_call_target="tpu_custom_call", output_to_operand_aliasing={{1}: (4, {}), {2}: (5, {})} | custom-call | flops 1000000000 | bytes 1048576 | tf_op jit(solution)/shard_map/pallas_call | solution.py:20
  15.9 0.4 %collective-permute-done.1.refs_1_ = f32[64,128]{1,0:T(8,128)S(1)} collective-permute-done((f32[64,128]{1,0:T(8,128)S(1)}, f32[64,128]{1,0:T(8,128)S(1)}, u32[]{:S(2)}, u32[]{:S(2)}) %collective-permute-start.1) | collective-permute-done | bytes 32800 | tf_op jit(solution)/shard_map/ppermute | solution.py:220
  16.3 0.0 collective-permute-done.4.refs_3_
  16.3 0.0 copy-done.6
  16.3 1.2 %shard_map.86 = bf16[8,32,128]{2,1,0:T(8,128)(2,1)} custom-call(f32[64,128]{1,0:T(8,128)S(1)} %get-tuple-element.13.refs_0_, f32[64,128]{1,0:T(8,128)S(1)} %collective-permute-done.1.refs_1_, f32[128,128]{1,0:T(8,128)S(1)} %collective-permute-done.3.refs_2_, f32[128,128]{1,0:T(8,128)S(1)} %collective-permute-done.4.refs_3_, ...), custom_call_target="tpu_custom_call" | custom-call | flops 1000000000 | bytes 1048576 | tf_op jit(solution)/shard_map/pallas_call | solution.py:20
  (2 shorter events, 0.0 us)
Async XLA Ops:
  0.0 1.7 %copy-start = (bf16[32,64,128]{2,1,0:T(8,128)(2,1)S(1)}, bf16[32,64,128]{2,1,0:T(8,128)(2,1)}, u32[]{:S(2)}) copy-start(bf16[32,64,128]{2,1,0:T(8,128)(2,1)} %pair_ref.1) | copy-start | bytes 1572868
  0.0 1.7 %copy-start.1 = (bf16[8,32,128]{2,1,0:T(8,128)(2,1)S(1)}, bf16[8,32,128]{2,1,0:T(8,128)(2,1)}, u32[]{:S(2)}) copy-start(bf16[8,32,128]{2,1,0:T(8,128)(2,1)} %param.9) | copy-start | bytes 196612
  0.0 1.7 %copy-start.7 = (f32[128,4]{0,1:T(4,128)S(1)}, f32[128,4]{0,1:T(4,128)}, u32[]{:S(2)}) copy-start(f32[128,4]{0,1:T(4,128)} %param.14) | copy-start | bytes 6148
  0.0 1.7 %collective-permute-start = (bf16[1,8,32,128]{3,2,1,0:T(8,128)(2,1)}, bf16[1,8,32,128]{3,2,1,0:T(8,128)(2,1)S(1)}, u32[]{:S(2)}, u32[]{:S(2)}) collective-permute-start(bf16[1,8,32,128]{3,2,1,0:T(8,128)(2,1)} %bitcast.2), channel_id=1, source_target_pairs={{0,4},{4,0},{8,12},{12,8},{16,20},{20,16},{24,28},{28,24},{1,5},{5... | collective-permute-start | bytes 196616 | tf_op jit(solution)/shard_map/ppermute | solution.py:206
  2.5 4.6 %collective-permute-start.2 = (f32[64,128]{1,0:T(8,128)S(1)}, f32[64,128]{1,0:T(8,128)S(1)}, u32[]{:S(2)}, u32[]{:S(2)}) collective-permute-start(f32[64,128]{1,0:T(8,128)S(1)} %get-tuple-element.13.refs_0_), channel_id=1, source_target_pairs={{0,4},{4,0},{8,12},{12,8},{16,20},{20,16},{24,28},{28,24},{1,5},{5... | collective-permute-start | bytes 98312 | tf_op jit(solution)/shard_map/ppermute | solution.py:206
  2.9 11.2 %collective-permute-start.5 = (bf16[1,8,32,128]{3,2,1,0:T(8,128)(2,1)S(1)}, bf16[1,8,32,128]{3,2,1,0:T(8,128)(2,1)S(1)}, u32[]{:S(2)}, u32[]{:S(2)}) collective-permute-start(bf16[1,8,32,128]{3,2,1,0:T(8,128)(2,1)S(1)} %bitcast.4), channel_id=1, source_target_pairs={{0,24},{4,28},{8,16},{12,20},{16,8},{20,12},{24,0},{28,4},{1,25},{... | collective-permute-start | bytes 196616 | tf_op jit(solution)/shard_map/ppermute | solution.py:211
  6.5 8.2 %copy-start.2 = (bf16[128,128]{1,0:T(8,128)(2,1)S(1)}, bf16[128,128]{1,0:T(8,128)(2,1)}, u32[]{:S(2)}) copy-start(bf16[128,128]{1,0:T(8,128)(2,1)} %refs_3_.2) | copy-start | bytes 98308
  6.5 8.2 %copy-start.3 = (bf16[128,128]{1,0:T(8,128)(2,1)S(1)}, bf16[128,128]{1,0:T(8,128)(2,1)}, u32[]{:S(2)}) copy-start(bf16[128,128]{1,0:T(8,128)(2,1)} %refs_4_.1) | copy-start | bytes 98308
  6.5 8.2 %copy-start.4 = (bf16[128,128]{1,0:T(8,128)(2,1)S(1)}, bf16[128,128]{1,0:T(8,128)(2,1)}, u32[]{:S(2)}) copy-start(bf16[128,128]{1,0:T(8,128)(2,1)} %refs_6_.1) | copy-start | bytes 98308
  6.5 8.2 %copy-start.5 = (bf16[128,128]{1,0:T(8,128)(2,1)S(1)}, bf16[128,128]{1,0:T(8,128)(2,1)}, u32[]{:S(2)}) copy-start(bf16[128,128]{1,0:T(8,128)(2,1)} %refs_3_.3) | copy-start | bytes 98308
  6.5 5.0 %collective-permute-start.7 = (bf16[2,8,32,128]{3,2,1,0:T(8,128)(2,1)S(1)}, bf16[2,8,32,128]{3,2,1,0:T(8,128)(2,1)S(1)}, u32[]{:S(2)}, u32[]{:S(2)}) collective-permute-start(bf16[2,8,32,128]{3,2,1,0:T(8,128)(2,1)S(1)} %get-tuple-element.14.refs_0_), channel_id=1, source_target_pairs={{0,16},{4,12},{8,24},{12,4},{16,0},{20,28},{24,8},{28,20},{1,17},{... | collective-permute-start | bytes 393224 | tf_op jit(solution)/shard_map/ppermute | solution.py:211
  7.1 7.3 %collective-permute-start.3 = (f32[128,128]{1,0:T(8,128)S(1)}, f32[128,128]{1,0:T(8,128)S(1)}, u32[]{:S(2)}, u32[]{:S(2)}) collective-permute-start(f32[128,128]{1,0:T(8,128)S(1)} %pad_maximum_fusion), channel_id=1, source_target_pairs={{0,1},{1,0},{2,3},{3,2},{4,7},{5,6},{6,5},{7,4},{8,9},{9,8},{10,11... | collective-permute-start | bytes 196616 | tf_op jit(solution)/shard_map/ppermute | solution.py:220
  11.5 3.9 %collective-permute-start.8 = (bf16[2,8,32,128]{3,2,1,0:T(8,128)(2,1)S(1)}, bf16[2,8,32,128]{3,2,1,0:T(8,128)(2,1)S(1)}, u32[]{:S(2)}, u32[]{:S(2)}) collective-permute-start(bf16[2,8,32,128]{3,2,1,0:T(8,128)(2,1)S(1)} %collective-permute-done.7.refs_2_), channel_id=1, source_target_pairs={{0,4},{4,0},{8,12},{12,8},{16,20},{20,16},{24,28},{28,24},{1,5},{5... | collective-permute-start | bytes 393224 | tf_op jit(solution)/shard_map/ppermute | solution.py:206
  11.5 4.8 %collective-permute-start.1 = (f32[64,128]{1,0:T(8,128)S(1)}, f32[64,128]{1,0:T(8,128)S(1)}, u32[]{:S(2)}, u32[]{:S(2)}) collective-permute-start(f32[64,128]{1,0:T(8,128)S(1)} %get-tuple-element.13.refs_0_), channel_id=1, source_target_pairs={{0,2},{1,3},{2,0},{3,1},{4,6},{5,7},{6,4},{7,5},{8,10},{9,11},{10,... | collective-permute-start | bytes 98312 | tf_op jit(solution)/shard_map/ppermute | solution.py:220
  14.1 1.3 %collective-permute-start.6 = (bf16[1,8,32,128]{3,2,1,0:T(8,128)(2,1)S(1)}, bf16[1,8,32,128]{3,2,1,0:T(8,128)(2,1)S(1)}, u32[]{:S(2)}, u32[]{:S(2)}) collective-permute-start(bf16[1,8,32,128]{3,2,1,0:T(8,128)(2,1)S(1)} %collective-permute-done.5.refs_1_), channel_id=1, source_target_pairs={{0,4},{4,0},{8,12},{12,8},{16,20},{20,16},{24,28},{28,24},{1,5},{5... | collective-permute-start | bytes 196616 | tf_op jit(solution)/shard_map/ppermute | solution.py:206
  14.3 2.0 %collective-permute-start.4 = (f32[128,128]{1,0:T(8,128)S(1)}, f32[128,128]{1,0:T(8,128)S(1)}, u32[]{:S(2)}, u32[]{:S(2)}) collective-permute-start(f32[128,128]{1,0:T(8,128)S(1)} %collective-permute-done.3.refs_2_), channel_id=1, source_target_pairs={{0,4},{4,0},{8,12},{12,8},{16,20},{20,16},{24,28},{28,24},{1,5},{5... | collective-permute-start | bytes 196616 | tf_op jit(solution)/shard_map/ppermute | solution.py:206
  15.4 1.0 %copy-start.6 = (bf16[128,128]{1,0:T(8,128)(2,1)S(1)}, bf16[128,128]{1,0:T(8,128)(2,1)}, u32[]{:S(2)}) copy-start(bf16[128,128]{1,0:T(8,128)(2,1)} %refs_7_.1) | copy-start | bytes 98308
